TPU v7x, 32 devices: a whole 2x2x4 slice. The times are simulated.
32 devices in a mesh: row: 8 (over z, x), col: 4 (over y, core).
Axes of the slice: x: 2, y: 2, z: 4, core: 2. Of those that a mesh axis runs over, the one named last changes fastest.
Arguments:
- source_points: bfloat16 [512, 64, 128], P(('row', 'col')), may hold values from -1.5 to 1.5
- target_points: bfloat16 [512, 64, 128], P(('row', 'col')), may hold values from -1.5 to 1.5
- source_mass: float32 [512, 128], P(('row', 'col')), may hold values from -4 to 4
- target_mass: float32 [512, 128], P(('row', 'col')), may hold values from -4 to 4
- support: int32 [512, 32], P(('row', 'col')), may hold values from 0 to 511, as said below
- coarse_potential: float32 [512, 128], P(('row', 'col')), may hold values from -4 to 150
Outputs:
- potential_f: float32 [512, 128], P(('row', 'col'))
- potential_g: float32 [512, 128], P(('row', 'col'))
Inputs may be any that keep to these rules, and one draw needn't show every extreme that they name: `support`: each row names 32 different target clusters. The rows of one device's 16 source clusters name, among the 16 target clusters of any one device, exactly 2 different ones. Every target cluster is named by some row.
All inputs are finite; a program needn't handle non-finite values.
Results may differ from a plain program's by a relative error of at most 0.0003.
Values may be sent and summed in bfloat16 or wider, within the bound.
A program may use at most 64 MiB of HBM per device.

v0:
```python
import functools

import jax
import jax.numpy as jnp
from jax import lax
from jax.experimental import pallas as pl
from jax.experimental.pallas import tpu as pltpu
from jax.sharding import PartitionSpec as P

CAP = 2
ITERS = 2
AXES = ("row", "col")
GROUP = 4
MESH = pl.DeviceIdType.MESH


epsilon = 0.5
lowest = -1e30


def squares(points):
    wide = points.astype(jnp.float32)
    return jnp.sum(wide * wide, axis=-2)


def pieces(row, depth):
    high = row.astype(jnp.bfloat16).astype(jnp.float32)
    rest = row - high
    middle = rest.astype(jnp.bfloat16).astype(jnp.float32)
    low = rest - middle
    index = lax.broadcasted_iota(jnp.int32, (depth, row.shape[1]), 0)
    return jnp.where(
        index == 0, high, jnp.where(index == 1, middle, jnp.where(index == 2, low, 0.0))
    )


def ones_rows(depth, points):
    index = lax.broadcasted_iota(jnp.int32, (depth, points), 0)
    return jnp.where(index < 3, 1.0, 0.0)


def fold(old_max, old_sum, scores):
    rows, lanes = scores.shape
    blocks = scores.reshape(rows // 8, 8, lanes)
    upper = jnp.maximum(old_max, jnp.max(blocks, axis=0))
    total = old_sum * jnp.exp(old_max - upper) + jnp.sum(jnp.exp(blocks - upper[None]), axis=0)
    return upper, total


def sweep_kernel(
    slots_ref, source_ref, mass_ref, tiles_ref, u_ref, row_ref, column_ref,
    tile_forward, tile_backward, run_max, run_sum,
):
    clusters, features, points = source_ref.shape
    slots = tiles_ref.shape[0]
    entries = slots_ref.shape[1]
    spare = tile_forward.shape[2] - features
    ones = ones_rows(spare, points)

    def prepare(slot, carry):
        tile = tiles_ref[slot].astype(jnp.float32)
        extra = pieces(u_ref[pl.ds(slot, 1), :], spare)
        tile_forward[slot] = jnp.concatenate([4.0 * tile, extra], axis=0).T.astype(jnp.bfloat16)
        tile_backward[slot] = jnp.concatenate([tile, ones], axis=0).astype(jnp.bfloat16)
        run_max[slot] = jnp.full((8, points), lowest, jnp.float32)
        run_sum[slot] = jnp.zeros((8, points), jnp.float32)
        return carry

    lax.fori_loop(0, slots, prepare, 0, unroll=8)

    def visit(cluster, carry):
        source = source_ref[cluster].astype(jnp.float32)
        right = jnp.concatenate([source, ones], axis=0).astype(jnp.bfloat16)

        def forward(step, state):
            lhs = jnp.concatenate(
                [tile_forward[slots_ref[cluster, step * GROUP + lane]] for lane in range(GROUP)],
                axis=0,
            )
            return fold(*state, jnp.dot(lhs, right, preferred_element_type=jnp.float32))

        start = (
            jnp.full((8, points), lowest, jnp.float32),
            jnp.zeros((8, points), jnp.float32),
        )
        upper, total = lax.fori_loop(0, entries // GROUP, forward, start, unroll=True)
        peak = jnp.max(upper, axis=0, keepdims=True)
        total = jnp.sum(total * jnp.exp(upper - peak), axis=0, keepdims=True)
        level = peak + jnp.log(total)
        row_ref[pl.ds(cluster, 1), :] = level
        extra = pieces(mass_ref[pl.ds(cluster, 1), :] - level, spare)
        left = jnp.concatenate([4.0 * source, extra], axis=0).T.astype(jnp.bfloat16)

        def backward(step, state):
            chosen = [slots_ref[cluster, step * GROUP + lane] for lane in range(GROUP)]
            held = [(run_max[slot], run_sum[slot]) for slot in chosen]
            rhs = jnp.concatenate([tile_backward[slot] for slot in chosen], axis=1)
            scores = jnp.dot(left, rhs, preferred_element_type=jnp.float32)
            fresh = [
                fold(*held[lane], scores[:, lane * points : (lane + 1) * points])
                for lane in range(GROUP)
            ]
            for slot, (new_max, new_sum) in zip(chosen, fresh):
                run_max[slot] = new_max
                run_sum[slot] = new_sum
            return state

        lax.fori_loop(0, entries // GROUP, backward, 0, unroll=True)
        return carry

    lax.fori_loop(0, clusters, visit, 0)
    upper = run_max[...]
    peak = jnp.max(upper, axis=1, keepdims=True)
    total = jnp.sum(run_sum[...] * jnp.exp(upper - peak), axis=1)
    column_ref[...] = peak[:, 0] + jnp.log(total)


def sweep_call(slot_list, source, mass, tiles, u):
    clusters, features, points = source.shape
    slots = tiles.shape[0]
    depth = 2 * features
    vmem = pl.BlockSpec(memory_space=pltpu.VMEM)
    pairs = clusters * slot_list.shape[1]
    return pl.pallas_call(
        sweep_kernel,
        out_shape=(
            jax.ShapeDtypeStruct((clusters, points), jnp.float32),
            jax.ShapeDtypeStruct((slots, points), jnp.float32),
        ),
        in_specs=[pl.BlockSpec(memory_space=pltpu.SMEM), vmem, vmem, vmem, vmem],
        out_specs=(vmem, vmem),
        scratch_shapes=[
            pltpu.VMEM((slots, points, depth), jnp.bfloat16),
            pltpu.VMEM((slots, depth, points), jnp.bfloat16),
            pltpu.VMEM((slots, 8, points), jnp.float32),
            pltpu.VMEM((slots, 8, points), jnp.float32),
        ],
        cost_estimate=pl.CostEstimate(
            flops=4 * pairs * points * points * depth,
            transcendentals=2 * pairs * points * points,
            bytes_accessed=2 * slots * features * points,
        ),
        name="sweep",
    )(slot_list, source, mass, tiles, u)


def place():
    rows, columns = lax.axis_size("row"), lax.axis_size("col")
    return lax.axis_index("row") * columns + lax.axis_index("col"), rows * columns, columns


def peer_of(step):
    me, devices, columns = place()
    peer = lax.rem(me + step, devices)
    return peer, (lax.div(peer, columns), lax.rem(peer, columns))


def greet():
    devices = place()[1]
    barrier = pltpu.get_barrier_semaphore()

    def signal(step, carry):
        pl.semaphore_signal(barrier, inc=1, device_id=peer_of(step)[1], device_id_type=MESH)
        return carry

    lax.fori_loop(1, devices, signal, 0, unroll=8)
    pl.semaphore_wait(barrier, devices - 1)


def send_all(sources, targets, send_sem, recv_sem, first):
    me, devices, _ = place()

    def send(step, carry):
        peer, where = peer_of(step)
        for index, (source, target) in enumerate(zip(sources, targets)):
            pltpu.make_async_remote_copy(
                src_ref=source.at[peer],
                dst_ref=target.at[me],
                send_sem=send_sem.at[first + index],
                recv_sem=recv_sem.at[first + index],
                device_id=where,
                device_id_type=MESH,
            ).start()
        return carry

    lax.fori_loop(1, devices, send, 0, unroll=8)
    for source, target in zip(sources, targets):
        target[me] = source[me]


def wait_all(refs, sems, first):
    devices = place()[1]
    for index, ref in enumerate(refs):
        blocks = ref.at[pl.ds(0, devices - 1)]
        pltpu.make_async_copy(blocks, blocks, sems.at[first + index]).wait()


def exchange_kernel(count, *refs):
    sources, targets = refs[:count], refs[count : 2 * count]
    send_sem, recv_sem = refs[2 * count :]
    greet()
    send_all(sources, targets, send_sem, recv_sem, 0)
    wait_all(targets, recv_sem, 0)
    wait_all(sources, send_sem, 0)


def exchange(arrays, collective_id):
    count = len(arrays)
    vmem = pl.BlockSpec(memory_space=pltpu.VMEM)
    return pl.pallas_call(
        functools.partial(exchange_kernel, count),
        out_shape=tuple(jax.ShapeDtypeStruct(array.shape, array.dtype) for array in arrays),
        in_specs=[vmem] * count,
        out_specs=(vmem,) * count,
        scratch_shapes=[pltpu.SemaphoreType.DMA((count,)), pltpu.SemaphoreType.DMA((count,))],
        compiler_params=pltpu.CompilerParams(collective_id=collective_id, has_side_effects=True),
        name="exchange" + str(collective_id),
    )(*arrays)


def combined(asked, parts, cluster):
    masked = jnp.where(asked == cluster, parts, lowest)
    upper = jnp.max(jnp.max(masked, axis=0), axis=0, keepdims=True)
    total = jnp.sum(jnp.sum(jnp.exp(masked - upper[None]), axis=0), axis=0, keepdims=True)
    return upper + jnp.log(total)


def turn_kernel(column_ref, asked_ref, mass_ref, u_ref, parts_ref, outgoing_ref, send_sem, recv_sem):
    greet()
    send_all([column_ref], [parts_ref], send_sem, recv_sem, 0)
    wait_all([parts_ref], recv_sem, 0)
    asked, parts = asked_ref[...], parts_ref[...]

    outgoing = jnp.zeros(parts.shape, jnp.float32)
    for cluster in range(mass_ref.shape[0]):
        row = mass_ref[cluster : cluster + 1, :] - combined(asked, parts, cluster)
        outgoing = jnp.where(asked == cluster, row[None], outgoing)
    outgoing_ref[...] = outgoing
    send_all([outgoing_ref], [u_ref], send_sem, recv_sem, 1)
    wait_all([u_ref], recv_sem, 1)
    wait_all([column_ref, outgoing_ref], send_sem, 0)


def finish_kernel(column_ref, asked_ref, level_ref, parts_ref, send_sem, recv_sem):
    greet()
    send_all([column_ref], [parts_ref], send_sem, recv_sem, 0)
    wait_all([parts_ref], recv_sem, 0)
    asked, parts = asked_ref[...], parts_ref[...]
    for cluster in range(level_ref.shape[0]):
        level_ref[cluster : cluster + 1, :] = combined(asked, parts, cluster)
    wait_all([column_ref], send_sem, 0)


def owner_call(kernel, out, scratch, collective_id, *operands):
    vmem = pl.BlockSpec(memory_space=pltpu.VMEM)
    return pl.pallas_call(
        kernel,
        out_shape=out,
        in_specs=[vmem] * len(operands),
        out_specs=vmem,
        scratch_shapes=scratch
        + [pltpu.SemaphoreType.DMA((2,)), pltpu.SemaphoreType.DMA((2,))],
        compiler_params=pltpu.CompilerParams(collective_id=collective_id, has_side_effects=True),
        name="owner" + str(collective_id),
    )(*operands)


def body(source_points, target_points, source_mass, target_mass, support, coarse_potential):
    devices = lax.axis_size(AXES)
    local_count, features, points = source_points.shape
    owner = support // local_count
    within = support % local_count
    flat_owner, flat_within = owner.reshape(-1), within.reshape(-1)
    named = flat_owner[None, :] == jnp.arange(devices, dtype=jnp.int32)[:, None]
    first = jnp.min(jnp.where(named, flat_within[None, :], local_count), axis=1)
    second = jnp.max(jnp.where(named, flat_within[None, :], -1), axis=1)
    request = jnp.stack([first, second], axis=1).astype(jnp.int32)
    shape = (devices, CAP, points)
    (asked,) = exchange([jnp.broadcast_to(request[:, :, None], shape)], 0)
    first_of = jnp.sum(jnp.where(named, first[:, None], 0), axis=0).reshape(owner.shape)
    slot_list = (owner * CAP + (within > first_of).astype(jnp.int32)).astype(jnp.int32)

    target_sq = squares(target_points)
    source_sq = squares(source_points)
    u = 2.0 * (coarse_potential - target_sq) + target_mass
    matches = asked[:, :, None, :] == jnp.arange(local_count, dtype=jnp.int32)[:, None]
    sending = jnp.sum(jnp.where(matches, u, 0.0), axis=2)
    tiles, received = exchange([target_points[asked[:, :, 0]], sending], 1)
    tiles = tiles.reshape(devices * CAP, features, points)
    row_shape = jax.ShapeDtypeStruct(shape, jnp.float32)
    level_shape = jax.ShapeDtypeStruct(target_mass.shape, jnp.float32)
    buffer = pltpu.VMEM(shape, jnp.float32)
    for sweep in range(ITERS):
        level, column = sweep_call(
            slot_list, source_points, source_mass, tiles, received.reshape(devices * CAP, points)
        )
        column = column.reshape(shape)
        if sweep < ITERS - 1:
            received = owner_call(
                turn_kernel, row_shape, [buffer, buffer], 2 + sweep, column, asked, target_mass
            )
    column_level = owner_call(finish_kernel, level_shape, [buffer], 1 + ITERS, column, asked)
    return (source_sq - 0.5 * level, target_sq - 0.5 * column_level)


def solution(mesh):
    placed = (
        P(AXES, None, None),
        P(AXES, None, None),
        P(AXES, None),
        P(AXES, None),
        P(AXES, None),
        P(AXES, None),
    )
    return jax.shard_map(
        body,
        mesh=mesh,
        in_specs=placed,
        out_specs=(P(AXES, None), P(AXES, None)),
        check_vma=False,
    )
```

profile of v0, /device:TPU:0, one launch (start us, length us, event | category | flops | bytes accessed | tf_op | source)
XLA Modules:
  0.0 126.4 jit_solution(15784694009997400920)
XLA Ops:
  0.6 0.7 add_select_fusion.1
  1.3 0.1 eq.30
  1.4 0.1 broadcast_in_dim.52
  1.5 0.1 select_reduce_fusion.1
  1.6 0.1 copy.10
  1.7 0.7 broadcast_in_dim.59.refs_0_
  2.4 10.7 %exchange0.1.asked_ref = s32[32,2,128]{2,1,0:T(2,128)} custom-call(s32[32,2,128]{2,1,0:T(2,128)} %broadcast_in_dim.59.refs_0_), custom_call_target="tpu_custom_call" | custom-call | tf_op jit(solution)/shard_map/exchange0/pallas_call | solution.py:210
  13.2 1.0 multiply_reduce_fusion
  14.2 0.7 copy-done.1
  15.0 0.7 select_reduce_fusion.refs_1_
  15.7 0.6 fusion
  16.4 0.1 reshape.35
  16.5 1.7 %gather_fusion = bf16[64,64,128]{2,1,0:T(8,128)(2,1)} fusion(bf16[16,64,128]{2,1,0:T(8,128)(2,1)S(1)} %copy-done, s32[1024]{0:T(1024)S(1)} %pad_clamp_fusion), kind=kCustom, calls=%fused_computation | custom fusion | bytes 2097408 | tf_op jit(solution)/shard_map/gather | solution.py:288
  18.2 25.3 %exchange1.1 = (bf16[32,2,64,128]{3,2,1,0:T(8,128)(2,1)}, f32[32,2,128]{2,1,0:T(2,128)}) custom-call(bf16[32,2,64,128]{3,2,1,0:T(8,128)(2,1)} %bitcast.8, f32[32,2,128]{2,1,0:T(2,128)} %select_reduce_fusion.refs_1_), custom_call_target="tpu_custom_call" | custom-call | tf_op jit(solution)/shard_map/exchange1/pallas_call | solution.py:210
  43.5 0.1 select_reduce_fusion.2
  43.6 0.1 reshape.27
  43.7 0.5 copy-done.3
  44.2 0.6 convert_add_fusion.slots_ref
  44.8 24.1 %sweep.2 = (f32[16,128]{1,0:T(8,128)}, f32[64,128]{1,0:T(8,128)}) custom-call(s32[16,32]{1,0:T(8,128)} %convert_add_fusion.slots_ref, bf16[16,64,128]{2,1,0:T(8,128)(2,1)} %source_ref.3, f32[16,128]{1,0:T(8,128)} %mass_ref.5, bf16[64,64,128]{2,1,0:T(8,128)(2,1)} %bitcast.14, f32[64,128]{1,0:T(8,128)} %bitcast.16), custom_call_target="tpu_custom_call" | custom-call | flops 4294967296 | bytes 1048576 | tf_op jit(solution)/shard_map/sweep/pallas_call | solution.py:124
  68.9 22.4 %owner2.1 = f32[32,2,128]{2,1,0:T(2,128)} custom-call(f32[32,2,128]{2,1,0:T(2,128)} %bitcast.11, s32[32,2,128]{2,1,0:T(2,128)} %exchange0.1.asked_ref, f32[16,128]{1,0:T(8,128)} %mass_ref.4), custom_call_target="tpu_custom_call" | custom-call | tf_op jit(solution)/shard_map/owner2/pallas_call | solution.py:256
  91.3 24.1 %sweep.3 = (f32[16,128]{1,0:T(8,128)}, f32[64,128]{1,0:T(8,128)}) custom-call(s32[16,32]{1,0:T(8,128)} %convert_add_fusion.slots_ref, bf16[16,64,128]{2,1,0:T(8,128)(2,1)} %source_ref.3, f32[16,128]{1,0:T(8,128)} %mass_ref.5, bf16[64,64,128]{2,1,0:T(8,128)(2,1)} %bitcast.15, f32[64,128]{1,0:T(8,128)} %bitcast.10), custom_call_target="tpu_custom_call" | custom-call | flops 4294967296 | bytes 1048576 | tf_op jit(solution)/shard_map/sweep/pallas_call | solution.py:124
  115.4 9.6 %owner3.1 = f32[16,128]{1,0:T(8,128)} custom-call(f32[32,2,128]{2,1,0:T(2,128)} %bitcast.9, s32[32,2,128]{2,1,0:T(2,128)} %exchange0.1.asked_ref), custom_call_target="tpu_custom_call" | custom-call | tf_op jit(solution)/shard_map/owner3/pallas_call | solution.py:256
  125.1 0.6 copy-done.4
  125.8 0.6 multiply_subtract_fusion
  (17 shorter events, 0.1 us)
Async XLA Ops:
  2.4 14.0 %copy-start = (bf16[16,64,128]{2,1,0:T(8,128)(2,1)S(1)}, bf16[16,64,128]{2,1,0:T(8,128)(2,1)}, u32[]{:S(2)}) copy-start(bf16[16,64,128]{2,1,0:T(8,128)(2,1)} %param.7) | copy-start | bytes 786436
  13.1 1.1 copy-start.5
  13.2 1.1 copy-start.6
  14.2 0.8 copy-start.1
  43.5 0.7 copy-start.3
  91.3 33.8 %copy-start.2 = (bf16[16,64,128]{2,1,0:T(8,128)(2,1)S(1)}, bf16[16,64,128]{2,1,0:T(8,128)(2,1)}, u32[]{:S(2)}) copy-start(bf16[16,64,128]{2,1,0:T(8,128)(2,1)} %source_ref.3) | copy-start | bytes 786436
  125.0 0.7 copy-start.4
  125.0 0.7 copy-start.7
where the time goes:
time: 127 us; the launch traced here: 126 us
  Pallas kernels  116 us (91%)
  local copies, waits for them, and re-layouts  4.74 us (4%)
  other arithmetic  4.63 us (4%)
    pallas_call x2, Pallas kernels, sweep_call(): pl.pallas_call(sweep_kernel, out_shape=(jax.ShapeDtypeStruct((clusters, p...  48.2 us
    pallas_call x2, Pallas kernels, exchange(): pl.pallas_call(functools.partial(exchange_kernel, count), out_shape=tuple...  36 us
    pallas_call x2, Pallas kernels, owner_call(): pl.pallas_call(kernel, out_shape=out, in_specs=[vmem] * len(operands), ou...  32 us

commit v1 on v0

--- a/solution.py
+++ b/solution.py
@@ -8,6 +8,10 @@
 from jax.sharding import PartitionSpec as P
 
 CAP = 2
+EXTRA = 16
+LIFT = 20.0
+FLOOR = 1e-10
+ALARM = 3e38
 ITERS = 2
 AXES = ("row", "col")
 GROUP = 4
@@ -265,21 +269,250 @@
     )(*operands)
 
 
-def body(source_points, target_points, source_mass, target_mass, support, coarse_potential):
-    devices = lax.axis_size(AXES)
+def bias_rows(row, ones_first):
+    high = row.astype(jnp.bfloat16).astype(jnp.float32)
+    rest = row - high
+    middle = rest.astype(jnp.bfloat16).astype(jnp.float32)
+    low = rest - middle
+    index = lax.broadcasted_iota(jnp.int32, (EXTRA, row.shape[1]), 0)
+    where, other = (3, 0) if ones_first else (0, 3)
+    ones = jnp.where((index >= other) & (index < other + 3), 1.0, 0.0)
+    return jnp.where(
+        index == where,
+        high,
+        jnp.where(index == where + 1, middle, jnp.where(index == where + 2, low, ones)),
+    )
+
+
+def split_rows(row):
+    high = row.astype(jnp.bfloat16).astype(jnp.float32)
+    index = lax.broadcasted_iota(jnp.int32, (16, row.shape[1]), 0)
+    return jnp.where(index == 0, high, jnp.where(index == 1, row - high, 0.0)).astype(jnp.bfloat16)
+
+
+def whole_max(array):
+    return jnp.max(jnp.max(array, axis=0, keepdims=True), axis=1, keepdims=True)
+
+
+def start_copy(source, target, sems, index, step):
+    me = place()[0]
+    peer, where = peer_of(step)
+    pltpu.make_async_remote_copy(
+        src_ref=source.at[peer],
+        dst_ref=target.at[me],
+        send_sem=sems[0].at[index],
+        recv_sem=sems[1].at[index],
+        device_id=where,
+        device_id_type=MESH,
+    ).start()
+
+
+def plan_kernel(
+    slots_ref, slot_row_ref, request_ref, source_ref, target_ref, mass_ref, target_mass_ref, coarse_ref,
+    f_ref, g_ref, flag_ref,
+    asked, asked_scalar, near, beta, tile_out, tiles, beta_out, betas, beta_next, columns, parts, columns_next, parts_next,
+    left, right, kernel_store, weight, level_f, rows, local_sem, send_sem, recv_sem,
+):
+    me, devices, _ = place()
+    clusters, features, points = source_ref.shape
+    entries = slots_ref.shape[1]
+    slots = devices * CAP
+    sems = (send_sem, recv_sem)
+    greet()
+    send_all([request_ref], [asked], send_sem, recv_sem, 0)
+
+    def prepare_source(cluster, carry):
+        wide = source_ref[cluster].astype(jnp.float32)
+        square = jnp.sum(wide * wide, axis=0, keepdims=True)
+        stacked = jnp.concatenate([4.0 * wide, bias_rows(LIFT - 2.0 * square, False)], axis=0)
+        left[cluster] = stacked.T.astype(jnp.bfloat16)
+        return carry
+
+    lax.fori_loop(0, clusters, prepare_source, 0, unroll=2)
+    near[...] = 2.0 * coarse_ref[...] + target_mass_ref[...]
+    wait_all([asked], recv_sem, 0)
+    scalars = pltpu.make_async_copy(asked, asked_scalar, local_sem.at[0])
+    scalars.start()
+    scalars.wait()
+
+    def serve(step, carry):
+        peer = peer_of(step)[0]
+        for entry in range(CAP):
+            chosen = asked_scalar[peer, entry, 0]
+            tile_out[peer, entry] = target_ref[chosen]
+            beta_out[peer, pl.ds(entry, 1), :] = near[pl.ds(chosen, 1), :]
+        start_copy(tile_out, tiles, sems, 1, step)
+        start_copy(beta_out, betas, sems, 2, step)
+        return carry
+
+    lax.fori_loop(1, devices, serve, 0, unroll=1)
+    for entry in range(CAP):
+        chosen = asked_scalar[me, entry, 0]
+        tiles[me, entry] = target_ref[chosen]
+        betas[me, pl.ds(entry, 1), :] = near[pl.ds(chosen, 1), :]
+    wait_all([betas], recv_sem, 2)
+    wait_all([tiles], recv_sem, 1)
+
+    def prepare_target(owner, carry):
+        for entry in range(CAP):
+            tile = tiles[owner, entry]
+            wide = tile.astype(jnp.float32)
+            square = jnp.sum(wide * wide, axis=0, keepdims=True)
+            extra = bias_rows(LIFT - 2.0 * square, True).astype(jnp.bfloat16)
+            right[owner * CAP + entry] = jnp.concatenate([tile, extra], axis=0)
+        return carry
+
+    lax.fori_loop(0, devices, prepare_target, 0, unroll=4)
+
+    def set_weights(values):
+        top = whole_max(values.reshape(slots, points))
+        weight[...] = jnp.exp(values.reshape(slots, points) - top)
+        return top
+
+    def close_row(cluster, total, top):
+        row = jnp.sum(total.T, axis=0, keepdims=True)
+        level_f[pl.ds(cluster, 1), :] = row
+
+    def build(cluster, carry):
+        total = jnp.zeros((points, points), jnp.float32)
+        for pair in range(entries // 2):
+            chosen = [slots_ref[cluster, 2 * pair + lane] for lane in range(2)]
+            rhs = jnp.concatenate([right[slot] for slot in chosen], axis=1)
+            values = jnp.exp(jnp.dot(left[cluster], rhs, preferred_element_type=jnp.float32))
+            kernel_store[cluster, :, pl.ds(pair * 2 * points, 2 * points)] = values.astype(jnp.bfloat16)
+            for lane, slot in enumerate(chosen):
+                total = total + values[:, lane * points : (lane + 1) * points] * weight[pl.ds(slot, 1), :]
+        close_row(cluster, total, carry)
+        return carry
+
+    def forward(cluster, carry):
+        total = jnp.zeros((points, points), jnp.float32)
+        for entry in range(entries):
+            values = kernel_store[cluster, :, pl.ds(entry * points, points)].astype(jnp.float32)
+            total = total + values * weight[pl.ds(slots_ref[cluster, entry], 1), :]
+        close_row(cluster, total, carry)
+        return carry
+
+    hot = jnp.where(
+        slot_row_ref[...] == lax.broadcasted_iota(jnp.int32, (slots, clusters * entries), 0), 1.0, 0.0
+    ).astype(jnp.bfloat16)
+
+    def backward(top):
+        sums = level_f[...]
+        level = jnp.log(sums) + (top - 2.0 * LIFT)
+        low = jnp.max(whole_max(jnp.where(sums >= FLOOR, 0.0, 1.0)), axis=0, keepdims=True)
+        level_f[...] = level
+        alpha = mass_ref[...] - level
+        peak = whole_max(alpha)
+
+        def visit(cluster, carry):
+            lifted = jnp.exp(mass_ref[pl.ds(cluster, 1), :] - level_f[pl.ds(cluster, 1), :] - peak)
+            products = jnp.dot(split_rows(lifted), kernel_store[cluster], preferred_element_type=jnp.float32)
+            row = products[0:1] + products[1:2]
+            for entry in range(entries):
+                rows[pl.ds(cluster * entries + entry, 1), :] = row[:, entry * points : (entry + 1) * points]
+            return carry
+
+        lax.fori_loop(0, clusters, visit, 0)
+        values = rows[...]
+        high = values.astype(jnp.bfloat16)
+        rest = values - high.astype(jnp.float32)
+        middle = rest.astype(jnp.bfloat16)
+        tail = (rest - middle.astype(jnp.float32)).astype(jnp.bfloat16)
+        total = jnp.dot(hot, high, preferred_element_type=jnp.float32)
+        total = total + jnp.dot(hot, middle, preferred_element_type=jnp.float32)
+        total = total + jnp.dot(hot, tail, preferred_element_type=jnp.float32)
+        low = jnp.maximum(low, whole_max(jnp.where(total >= FLOOR, 0.0, 1.0)))
+        column = jnp.log(total) + (peak - 2.0 * LIFT)
+        return jnp.where(low > 0.0, ALARM, column).reshape(devices, CAP, points)
+
+    top = set_weights(betas[...])
+    lax.fori_loop(0, clusters, build, 0)
+    columns[...] = backward(top)
+    send_all([columns], [parts], send_sem, recv_sem, 3)
+    wait_all([parts], recv_sem, 3)
+    for cluster in range(clusters):
+        near[cluster : cluster + 1, :] = target_mass_ref[cluster : cluster + 1, :] - combined(
+            asked[...], parts[...], cluster
+        )
+
+    def answer(step, carry):
+        peer = peer_of(step)[0]
+        for entry in range(CAP):
+            beta_out[peer, pl.ds(entry, 1), :] = near[pl.ds(asked_scalar[peer, entry, 0], 1), :]
+        start_copy(beta_out, beta_next, sems, 4, step)
+        return carry
+
+    wait_all([beta_out], send_sem, 2)
+    lax.fori_loop(1, devices, answer, 0, unroll=1)
+    for entry in range(CAP):
+        beta_next[me, pl.ds(entry, 1), :] = near[pl.ds(asked_scalar[me, entry, 0], 1), :]
+    wait_all([beta_next], recv_sem, 4)
+    top = set_weights(beta_next[...])
+    lax.fori_loop(0, clusters, forward, 0)
+    columns_next[...] = backward(top)
+    send_all([columns_next], [parts_next], send_sem, recv_sem, 5)
+    f_ref[...] = -0.5 * level_f[...]
+    wait_all([parts_next], recv_sem, 5)
+    for cluster in range(clusters):
+        g_ref[cluster : cluster + 1, :] = -0.5 * combined(asked[...], parts_next[...], cluster)
+    alarm = jnp.maximum(parts[...].reshape(slots, points), parts_next[...].reshape(slots, points))
+    flag_ref[...] = jnp.broadcast_to(
+        whole_max(jnp.where(alarm < 1e30, 0.0, 1.0)), flag_ref.shape
+    )
+    wait_all([request_ref], send_sem, 0)
+    wait_all([tile_out], send_sem, 1)
+    wait_all([columns], send_sem, 3)
+    wait_all([beta_out], send_sem, 4)
+    wait_all([columns_next], send_sem, 5)
+
+
+def plan_call(slot_list, request, source, target, mass, target_mass, coarse):
+    devices = request.shape[0]
+    clusters, features, points = source.shape
+    entries = slot_list.shape[1]
+    slots = devices * CAP
+    depth = features + EXTRA
+    vmem = pl.BlockSpec(memory_space=pltpu.VMEM)
+    row_block = pltpu.VMEM((devices, CAP, points), jnp.float32)
+    tile_block = pltpu.VMEM((devices, CAP, features, points), jnp.bfloat16)
+    sems = pltpu.SemaphoreType.DMA((6,))
+    return pl.pallas_call(
+        plan_kernel,
+        out_shape=(
+            jax.ShapeDtypeStruct((clusters, points), jnp.float32),
+            jax.ShapeDtypeStruct((clusters, points), jnp.float32),
+            jax.ShapeDtypeStruct((8, points), jnp.float32),
+        ),
+        in_specs=[pl.BlockSpec(memory_space=pltpu.SMEM)] + [vmem] * 7,
+        out_specs=(vmem, vmem, vmem),
+        scratch_shapes=[
+            pltpu.VMEM((devices, CAP, points), jnp.int32),
+            pltpu.SMEM((devices, CAP, points), jnp.int32),
+            pltpu.VMEM((clusters, points), jnp.float32),
+            pltpu.VMEM((clusters, points), jnp.float32),
+            tile_block, tile_block,
+            row_block, row_block, row_block, row_block, row_block, row_block, row_block,
+            pltpu.VMEM((clusters, points, depth), jnp.bfloat16),
+            pltpu.VMEM((slots, depth, points), jnp.bfloat16),
+            pltpu.VMEM((clusters, points, entries * points), jnp.bfloat16),
+            pltpu.VMEM((slots, points), jnp.float32),
+            pltpu.VMEM((clusters, points), jnp.float32),
+            pltpu.VMEM((clusters * entries, points), jnp.float32),
+            pltpu.SemaphoreType.DMA((1,)), sems, sems,
+        ],
+        compiler_params=pltpu.CompilerParams(
+            collective_id=8, has_side_effects=True, vmem_limit_bytes=60 * 1024 * 1024
+        ),
+        name="plan",
+    )(slot_list, slot_list.reshape(1, -1), request, source, target, mass, target_mass, coarse)
+
+
+def careful(slot_list, request, source_points, target_points, source_mass, target_mass, coarse_potential):
+    devices = request.shape[0]
     local_count, features, points = source_points.shape
-    owner = support // local_count
-    within = support % local_count
-    flat_owner, flat_within = owner.reshape(-1), within.reshape(-1)
-    named = flat_owner[None, :] == jnp.arange(devices, dtype=jnp.int32)[:, None]
-    first = jnp.min(jnp.where(named, flat_within[None, :], local_count), axis=1)
-    second = jnp.max(jnp.where(named, flat_within[None, :], -1), axis=1)
-    request = jnp.stack([first, second], axis=1).astype(jnp.int32)
     shape = (devices, CAP, points)
-    (asked,) = exchange([jnp.broadcast_to(request[:, :, None], shape)], 0)
-    first_of = jnp.sum(jnp.where(named, first[:, None], 0), axis=0).reshape(owner.shape)
-    slot_list = (owner * CAP + (within > first_of).astype(jnp.int32)).astype(jnp.int32)
-
+    (asked,) = exchange([request], 0)
     target_sq = squares(target_points)
     source_sq = squares(source_points)
     u = 2.0 * (coarse_potential - target_sq) + target_mass
@@ -303,6 +536,31 @@
     return (source_sq - 0.5 * level, target_sq - 0.5 * column_level)
 
 
+def body(source_points, target_points, source_mass, target_mass, support, coarse_potential):
+    devices = lax.axis_size(AXES)
+    local_count, features, points = source_points.shape
+    owner = support // local_count
+    within = support % local_count
+    flat_owner, flat_within = owner.reshape(-1), within.reshape(-1)
+    named = flat_owner[None, :] == jnp.arange(devices, dtype=jnp.int32)[:, None]
+    first = jnp.min(jnp.where(named, flat_within[None, :], local_count), axis=1)
+    second = jnp.max(jnp.where(named, flat_within[None, :], -1), axis=1)
+    request = jnp.stack([first, second], axis=1).astype(jnp.int32)
+    request = jnp.broadcast_to(request[:, :, None], (devices, CAP, points))
+    first_of = jnp.sum(jnp.where(named, first[:, None], 0), axis=0).reshape(owner.shape)
+    slot_list = (owner * CAP + (within > first_of).astype(jnp.int32)).astype(jnp.int32)
+    f, g, flag = plan_call(
+        slot_list, request, source_points, target_points, source_mass, target_mass, coarse_potential
+    )
+
+    def again():
+        return careful(
+            slot_list, request, source_points, target_points, source_mass, target_mass, coarse_potential
+        )
+
+    return lax.cond(flag[0, 0] > 0.0, again, lambda: (f, g))
+
+
 def solution(mesh):
     placed = (
         P(AXES, None, None),

time: 127 us -> 86.9 us (0.68)
  Pallas kernels: 116 us -> 79.5 us
  other arithmetic: 4.63 us -> 0.95 us
    pallas_call x6 -> x1, Pallas kernels: 116 us -> 79.5 us  [plan_call(): pl.pallas_call(plan_kernel, out_shape=(jax.ShapeDtypeStruct((clusters, po...]
    reduce_sum x3 -> x0, other arithmetic: 1.84 us -> none  [the longest x2 1.1 us: squares(): return jnp.sum(wide * wide, axis=-2)]
    gather x1 -> x0, local copies, waits for them, and re-layouts: 1.71 us -> none  [body(): tiles, received = exchange([target_points[asked[:, :, 0]], sending], 1)]
where the time goes in v1:
time: 86.9 us; the launch traced here: 86.5 us
  Pallas kernels  79.5 us (91%)
  local copies, waits for them, and re-layouts  4.61 us (5%)
  between operations  1.35 us (2%)
  other arithmetic  0.95 us (1%)
    pallas_call x1, Pallas kernels, plan_call(): pl.pallas_call(plan_kernel, out_shape=(jax.ShapeDtypeStruct((clusters, po...  79.5 us
    unnamed x14, local copies, waits for them, and re-layouts  2.35 us

profile of v1, /device:TPU:0, one launch (start us, length us, event | category | flops | bytes accessed | tf_op | source)
XLA Modules:
  0.0 86.5 jit_solution(12956130644016076250)
XLA Ops:
  0.6 0.7 add_select_fusion.1
  1.3 0.1 eq.30
  1.4 0.1 broadcast_in_dim.53
  1.5 0.1 select_reduce_fusion.1
  1.6 0.0 copy-start.5
  1.6 0.1 select_reduce_fusion.2
  1.7 0.1 reshape.34
  1.8 0.5 copy-done.5
  2.3 0.7 reshape.35.slot_row_ref
  3.0 0.1 copy.14
  3.1 0.0 copy-start.3
  3.1 0.0 copy-start.4
  3.1 0.0 copy-start.6
  3.1 0.1 broadcast_in_dim.60.request_ref
  3.2 0.6 copy-done.3
  3.8 0.0 copy-done.4
  3.8 0.0 copy-done.6
  3.8 0.0 copy-start
  3.8 79.5 %plan.1 = (f32[16,128]{1,0:T(8,128)S(1)}, f32[16,128]{1,0:T(8,128)S(1)}, f32[8,128]{1,0:T(8,128)}) custom-call(s32[16,32]{1,0:T(8,128)S(1)} %convert_add_fusion.slots_ref, s32[1,512]{1,0:T(1,128)} %reshape.35.slot_row_ref, s32[32,2,128]{2,1,0:T(2,128)S(1)} %broadcast_in_dim.60.request_ref, bf16[16,64,128]{2,1,0:T(8,128)(2,1)} %source_ref.1, ...), custom_call_target="tpu_custom_call" | custom-call | tf_op jit(solution)/shard_map/plan/pallas_call | solution.py:480
  83.4 1.2 %slice.6 = f32[1,1]{1,0:T(1,128)} slice(f32[8,128]{1,0:T(8,128)} %get-tuple-element.35), slice={[0:1], [0:1]} | slice | bytes 8 | tf_op jit(solution)/shard_map/slice | solution.py:561
  85.2 0.0 copy-done
  85.2 0.0 copy-done.1
  85.3 0.6 copy.21
  85.9 0.6 copy.22
  (4 shorter events, 0.0 us)
Async XLA Ops:
  1.6 0.7 copy-start.5
  3.1 0.7 copy-start.3
  3.1 0.7 copy-start.4
  3.1 0.7 copy-start.6
  3.8 81.4 %copy-start = (bf16[16,64,128]{2,1,0:T(8,128)(2,1)S(1)}, bf16[16,64,128]{2,1,0:T(8,128)(2,1)}, u32[]{:S(2)}) copy-start(bf16[16,64,128]{2,1,0:T(8,128)(2,1)} %target_ref.1) | copy-start | bytes 786436
  3.8 81.4 %copy-start.1 = (bf16[16,64,128]{2,1,0:T(8,128)(2,1)S(1)}, bf16[16,64,128]{2,1,0:T(8,128)(2,1)}, u32[]{:S(2)}) copy-start(bf16[16,64,128]{2,1,0:T(8,128)(2,1)} %source_ref.1) | copy-start | bytes 786436

commit v2 on v0

--- a/solution.py
+++ b/solution.py
@@ -8,6 +8,11 @@
 from jax.sharding import PartitionSpec as P
 
 CAP = 2
+EXTRA = 16
+LIFT = 20.0
+FLOOR = 1e-10
+ALARM = 3e38
+SENDS = 10
 ITERS = 2
 AXES = ("row", "col")
 GROUP = 4
@@ -265,7 +270,387 @@
     )(*operands)
 
 
-def body(source_points, target_points, source_mass, target_mass, support, coarse_potential):
+def bias_rows(row, ones_first):
+    high = row.astype(jnp.bfloat16).astype(jnp.float32)
+    rest = row - high
+    middle = rest.astype(jnp.bfloat16).astype(jnp.float32)
+    low = rest - middle
+    index = lax.broadcasted_iota(jnp.int32, (EXTRA, row.shape[1]), 0)
+    where, other = (3, 0) if ones_first else (0, 3)
+    ones = jnp.where((index >= other) & (index < other + 3), 1.0, 0.0)
+    return jnp.where(
+        index == where,
+        high,
+        jnp.where(index == where + 1, middle, jnp.where(index == where + 2, low, ones)),
+    )
+
+
+def split_rows(row):
+    high = row.astype(jnp.bfloat16).astype(jnp.float32)
+    index = lax.broadcasted_iota(jnp.int32, (16, row.shape[1]), 0)
+    return jnp.where(index == 0, high, jnp.where(index == 1, row - high, 0.0)).astype(jnp.bfloat16)
+
+
+def whole_max(array):
+    return jnp.max(jnp.max(array, axis=0, keepdims=True), axis=1, keepdims=True)
+
+
+def halves():
+    me, devices, columns = place()
+    half = devices // 2
+    side = lax.div(me, half)
+    return side, me - side * half, half, columns
+
+
+def block_of(step):
+    side, mine, half, columns = halves()
+    other = lax.div(step, half)
+    near = lax.rem(mine + lax.rem(step, half), half)
+    device = lax.rem(side + other, 2) * half + near
+    return other * half + near, near, (lax.div(device, columns), lax.rem(device, columns))
+
+
+def start_copy(source, target, sems, index, where):
+    pltpu.make_async_remote_copy(
+        src_ref=source,
+        dst_ref=target,
+        send_sem=sems[0].at[index],
+        recv_sem=sems[1].at[index],
+        device_id=where,
+        device_id_type=MESH,
+    ).start()
+
+
+def wait_blocks(ref, count, sem):
+    blocks = ref if count is None else ref.at[pl.ds(0, count)]
+    pltpu.make_async_copy(blocks, blocks, sem).wait()
+
+
+def plan_kernel(
+    support_ref, names_ref, source_ref, target_ref, mass_ref, target_mass_ref, coarse_ref,
+    f_ref, g_ref, flag_ref,
+    codes, codes_scalar, asked_near, asked_far, asked_scalar, slots_ref,
+    near, mate, mate_near, tile_out, mate_out, tiles, mate_tiles,
+    beta_out, mate_beta_out, betas, mate_betas, beta_next_out, beta_next,
+    columns, parts, columns_next, parts_next,
+    left, right, store_even, store_odd, weight, sums, level_f, peaks, lifted, hot, rows,
+    local_sem, send_sem, recv_sem,
+):
+    me, devices, _ = place()
+    side, mine, half, _ = halves()
+    clusters, features, points = source_ref.shape
+    entries = support_ref.shape[1]
+    slots = devices * CAP
+    sems = (send_sem, recv_sem)
+    barrier = pltpu.get_barrier_semaphore()
+
+    def signal(step, carry):
+        pl.semaphore_signal(barrier, inc=1, device_id=block_of(step)[2], device_id_type=MESH)
+        return carry
+
+    lax.fori_loop(1, devices, signal, 0, unroll=8)
+
+    block = lax.broadcasted_iota(jnp.int32, (devices, entries), 0)
+    far = jnp.where(block >= half, 1, 0)
+    owner_of_block = jnp.where(far == 1, 1 - side, side) * half + block - far * half
+    first = jnp.full((devices, entries), clusters, jnp.int32)
+    second = jnp.full((devices, entries), -1, jnp.int32)
+    for cluster in range(clusters):
+        name = names_ref[cluster : cluster + 1, :]
+        within = name - owner_of_block * clusters
+        named = (within >= 0) & (within < clusters)
+        first = jnp.minimum(first, jnp.where(named, within, clusters))
+        second = jnp.maximum(second, jnp.where(named, within, -1))
+    first = jnp.min(first, axis=1, keepdims=True)
+    second = jnp.max(second, axis=1, keepdims=True)
+    own = jnp.broadcast_to(first * clusters + second, (devices, points))
+    swapped = jnp.concatenate([own[half:], own[:half]], axis=0)
+    lane = lax.broadcasted_iota(jnp.int32, (devices, points), 1)
+    codes[...] = jnp.where(lane < points // 2, own, swapped).reshape(devices, 1, points)
+    slot_block = lax.broadcasted_iota(jnp.int32, (slots, entries), 0)
+    pair_first = jnp.broadcast_to(first.reshape(devices, 1, 1), (devices, CAP, entries)).reshape(slots, entries)
+    pair_second = jnp.broadcast_to(second.reshape(devices, 1, 1), (devices, CAP, entries)).reshape(slots, entries)
+    slot_device = lax.div(slot_block, CAP)
+    slot_far = jnp.where(slot_device >= half, 1, 0)
+    slot_owner = jnp.where(slot_far == 1, 1 - side, side) * half + slot_device - slot_far * half
+    slot_name = slot_owner * clusters + jnp.where(lax.rem(slot_block, CAP) == 0, pair_first, pair_second)
+    near[...] = 2.0 * coarse_ref[...] + target_mass_ref[...]
+    pl.semaphore_wait(barrier, devices - 1)
+
+    def ask(step, carry):
+        to, _, where = block_of(step)
+        start_copy(codes.at[to], asked_near.at[mine], sems, 0, where)
+        return carry
+
+    def ask_far(step, carry):
+        to, _, where = block_of(step)
+        start_copy(codes.at[to], asked_far.at[mine], sems, 1, where)
+        return carry
+
+    lax.fori_loop(1, half, ask, 0, unroll=5)
+    mate_where = block_of(half)[2]
+    start_copy(target_ref, mate, sems, 2, mate_where)
+    start_copy(near, mate_near, sems, 3, mate_where)
+    lax.fori_loop(half, devices, ask_far, 0, unroll=8)
+    local = pltpu.make_async_copy(codes, codes_scalar, local_sem.at[0])
+    local.start()
+
+    def prepare_source(cluster, carry):
+        wide = source_ref[cluster].astype(jnp.float32)
+        square = jnp.sum(wide * wide, axis=0, keepdims=True)
+        stacked = jnp.concatenate([4.0 * wide, bias_rows(LIFT - 2.0 * square, False)], axis=0)
+        left[cluster] = stacked.T.astype(jnp.bfloat16)
+        return carry
+
+    local.wait()
+    asked_near[mine] = codes[mine]
+    wait_blocks(asked_near, half - 1, recv_sem.at[0])
+    scalars = pltpu.make_async_copy(asked_near, asked_scalar, local_sem.at[1])
+    scalars.start()
+    scalars.wait()
+
+    def serve(origin, origin_near, tile_to, beta_to, tile_in, beta_in, lane, index):
+        def one(step, carry):
+            to, near_index, where = block_of(step)
+            code = asked_scalar[near_index, 0, lane]
+            chosen = lax.div(code, clusters)
+            for entry, pick in enumerate((chosen, code - chosen * clusters)):
+                tile_to[near_index, entry] = origin[pick]
+                beta_to[near_index, pl.ds(entry, 1), :] = origin_near[pl.ds(pick, 1), :]
+            start_copy(tile_to.at[near_index], tile_in.at[mine], sems, index, where)
+            start_copy(beta_to.at[near_index], beta_in.at[mine], sems, index + 1, where)
+            return carry
+
+        lax.fori_loop(1, half, one, 0)
+        code = asked_scalar[mine, 0, lane]
+        chosen = lax.div(code, clusters)
+        for entry, pick in enumerate((chosen, code - chosen * clusters)):
+            tile_in[mine, entry] = origin[pick]
+            beta_in[mine, pl.ds(entry, 1), :] = origin_near[pl.ds(pick, 1), :]
+
+    serve(target_ref, near, tile_out, beta_out, tiles, betas, 0, 4)
+    lax.fori_loop(0, clusters, prepare_source, 0, unroll=2)
+
+    def place_slots(cluster, carry):
+        for entry in range(entries):
+            name = support_ref[cluster, entry]
+            owner = lax.div(name, clusters)
+            owner_side = lax.div(owner, half)
+            to = lax.rem(owner_side + side, 2) * half + owner - owner_side * half
+            late = name - owner * clusters > lax.div(codes_scalar[to, 0, 0], clusters)
+            slots_ref[cluster, entry] = to * CAP + late.astype(jnp.int32)
+        return carry
+
+    lax.fori_loop(0, clusters, place_slots, 0)
+    for cluster in range(clusters):
+        hot[:, cluster * entries : (cluster + 1) * entries] = jnp.where(
+            names_ref[cluster : cluster + 1, :] == slot_name, 1.0, 0.0
+        )
+    wait_blocks(mate, None, recv_sem.at[2])
+    wait_blocks(mate_near, None, recv_sem.at[3])
+    serve(mate, mate_near, mate_out, mate_beta_out, mate_tiles, mate_betas, points // 2, 6)
+
+    def prepare_target(source, offset):
+        def one(owner, carry):
+            for entry in range(CAP):
+                tile = source[owner, entry]
+                wide = tile.astype(jnp.float32)
+                square = jnp.sum(wide * wide, axis=0, keepdims=True)
+                extra = bias_rows(LIFT - 2.0 * square, True).astype(jnp.bfloat16)
+                right[offset + owner * CAP + entry] = jnp.concatenate([tile, extra], axis=0)
+            return carry
+
+        lax.fori_loop(0, half, one, 0, unroll=4)
+
+    wait_blocks(betas, half - 1, recv_sem.at[5])
+    wait_blocks(tiles, half - 1, recv_sem.at[4])
+    prepare_target(tiles, 0)
+    wait_blocks(mate_betas, half - 1, recv_sem.at[7])
+    wait_blocks(mate_tiles, half - 1, recv_sem.at[6])
+    prepare_target(mate_tiles, half * CAP)
+    wait_blocks(asked_far, half, recv_sem.at[1])
+    asked_own = jnp.concatenate([asked_near[...], asked_far[...]], axis=0)[:, :, 0:1]
+    asked_code = jnp.broadcast_to(asked_own, (devices, CAP, points))
+    asked_first = lax.div(asked_code, clusters)
+    asked = jnp.where(
+        lax.broadcasted_iota(jnp.int32, (devices, CAP, points), 1) == 0,
+        asked_first,
+        asked_code - asked_first * clusters,
+    )
+
+    def set_weights(values):
+        top = whole_max(values)
+        weight[...] = jnp.exp(values - top)
+        return top
+
+    def close(cluster, total, top):
+        row = jnp.sum(total.T, axis=0, keepdims=True)
+        level = jnp.log(row) + (top - 2.0 * LIFT)
+        alpha = mass_ref[pl.ds(cluster, 1), :] - level
+        peak = jnp.max(alpha, axis=1, keepdims=True)
+        sums[pl.ds(cluster, 1), :] = row
+        level_f[pl.ds(cluster, 1), :] = level
+        peaks[pl.ds(cluster, 1), :] = jnp.broadcast_to(peak, (1, points))
+        lifted[cluster] = split_rows(jnp.exp(alpha - peak))
+
+    def build(cluster, store, index, pair, total):
+        chosen = [slots_ref[cluster, 2 * pair + lane] for lane in range(2)]
+        rhs = jnp.concatenate([right[slot] for slot in chosen], axis=1)
+        values = jnp.exp(jnp.dot(left[cluster], rhs, preferred_element_type=jnp.float32))
+        store[index, :, pl.ds(pair * 2 * points, 2 * points)] = values.astype(jnp.bfloat16)
+        for lane, slot in enumerate(chosen):
+            total = total + values[:, lane * points : (lane + 1) * points] * weight[pl.ds(slot, 1), :]
+        return total
+
+    def forward(cluster, store, index, pair, total):
+        for lane in range(2):
+            entry = 2 * pair + lane
+            values = store[index, :, pl.ds(entry * points, points)].astype(jnp.float32)
+            total = total + values * weight[pl.ds(slots_ref[cluster, entry], 1), :]
+        return total
+
+    def backward(cluster, store, index, pair):
+        products = jnp.dot(
+            lifted[cluster],
+            store[index, :, pl.ds(pair * 2 * points, 2 * points)],
+            preferred_element_type=jnp.float32,
+        )
+        row = products[0:1] + products[1:2]
+        for lane in range(2):
+            rows[pl.ds(cluster * entries + 2 * pair + lane, 1), :] = row[:, lane * points : (lane + 1) * points]
+
+    def sweep(make, top):
+        def mixed(cluster, store, index, before, old_store, old_index):
+            total = jnp.zeros((points, points), jnp.float32)
+            for pair in range(entries // 2):
+                if before is not None:
+                    backward(before, old_store, old_index, pair)
+                if cluster is not None:
+                    total = make(cluster, store, index, pair, total)
+            if cluster is not None:
+                close(cluster, total, top)
+
+        def both(index, carry):
+            mixed(2 * index + 1, store_odd, index, 2 * index, store_even, index)
+            mixed(2 * index + 2, store_even, index + 1, 2 * index + 1, store_odd, index)
+            return carry
+
+        last = clusters // 2 - 1
+        mixed(0, store_even, 0, None, None, None)
+        lax.fori_loop(0, last, both, 0)
+        mixed(clusters - 1, store_odd, last, clusters - 2, store_even, last)
+        mixed(None, None, None, clusters - 1, store_odd, last)
+        peak = whole_max(peaks[...])
+        scale = jnp.exp(peaks[...] - peak)
+        total = jnp.zeros((slots, points), jnp.float32)
+        values = jnp.concatenate(
+            [
+                rows[pl.ds(cluster * entries, entries), :] * scale[cluster : cluster + 1, :]
+                for cluster in range(clusters)
+            ],
+            axis=0,
+        )
+        choice = hot[...].astype(jnp.bfloat16)
+        for _ in range(3):
+            piece = values.astype(jnp.bfloat16)
+            total = total + jnp.dot(choice, piece, preferred_element_type=jnp.float32)
+            values = values - piece.astype(jnp.float32)
+        low = jnp.maximum(
+            whole_max(jnp.where(sums[...] >= FLOOR, 0.0, 1.0)), whole_max(jnp.where(total >= FLOOR, 0.0, 1.0))
+        )
+        column = jnp.log(total) + (peak - 2.0 * LIFT)
+        return jnp.where(low > 0.0, ALARM, column).reshape(devices, CAP, points)
+
+    def return_columns(source, target, index):
+        def one(step, carry):
+            to, near_index, where = block_of(step)
+            landing = lax.div(to, half) * half + mine
+            start_copy(source.at[to], target.at[landing], sems, index, where)
+            return carry
+
+        lax.fori_loop(1, devices, one, 0, unroll=8)
+        target[mine] = source[mine]
+        wait_blocks(target, devices - 1, recv_sem.at[index])
+
+    start = jnp.concatenate([betas[...], mate_betas[...]], axis=0).reshape(slots, points)
+    columns[...] = sweep(build, set_weights(start))
+    return_columns(columns, parts, 8)
+    for cluster in range(clusters):
+        near_row = target_mass_ref[cluster : cluster + 1, :] - combined(asked, parts[...], cluster)
+        beta_next_out[...] = jnp.where(asked == cluster, near_row[None], beta_next_out[...] if cluster else 0.0)
+    return_columns(beta_next_out, beta_next, 9)
+    columns_next[...] = sweep(forward, set_weights(beta_next[...].reshape(slots, points)))
+    f_ref[...] = level_f[...]
+    return_columns(columns_next, parts_next, 10)
+    for cluster in range(clusters):
+        g_ref[cluster : cluster + 1, :] = combined(asked, parts_next[...], cluster)
+    alarm = jnp.maximum(parts[...].reshape(slots, points), parts_next[...].reshape(slots, points))
+    flag_ref[...] = jnp.broadcast_to(whole_max(jnp.where(alarm < 1e30, 0.0, 1.0)), flag_ref.shape)
+    wait_blocks(codes, half - 1, send_sem.at[0])
+    wait_blocks(codes, half, send_sem.at[1])
+    wait_blocks(mate, None, send_sem.at[2])
+    wait_blocks(near, None, send_sem.at[3])
+    wait_blocks(tile_out, half - 1, send_sem.at[4])
+    wait_blocks(beta_out, half - 1, send_sem.at[5])
+    wait_blocks(mate_out, half - 1, send_sem.at[6])
+    wait_blocks(mate_beta_out, half - 1, send_sem.at[7])
+    wait_blocks(columns, devices - 1, send_sem.at[8])
+    wait_blocks(beta_next_out, devices - 1, send_sem.at[9])
+    wait_blocks(columns_next, devices - 1, send_sem.at[10])
+
+
+def plan_call(support, source, target, mass, target_mass, coarse):
+    devices = lax.axis_size(AXES)
+    clusters, features, points = source.shape
+    entries = support.shape[1]
+    slots = devices * CAP
+    half = devices // 2
+    depth = features + EXTRA
+    vmem = pl.BlockSpec(memory_space=pltpu.VMEM)
+    level = jax.ShapeDtypeStruct((clusters, points), jnp.float32)
+    levels = pltpu.VMEM((clusters, points), jnp.float32)
+    row_block = pltpu.VMEM((devices, CAP, points), jnp.float32)
+    half_row = pltpu.VMEM((half, CAP, points), jnp.float32)
+    half_tile = pltpu.VMEM((half, CAP, features, points), jnp.bfloat16)
+    half_code = pltpu.VMEM((half, 1, points), jnp.int32)
+    kernel_block = pltpu.VMEM((clusters // 2, points, entries * points), jnp.bfloat16)
+    sems = pltpu.SemaphoreType.DMA((11,))
+    return pl.pallas_call(
+        plan_kernel,
+        out_shape=(level, level, jax.ShapeDtypeStruct((8, points), jnp.float32)),
+        in_specs=[pl.BlockSpec(memory_space=pltpu.SMEM)] + [vmem] * 6,
+        out_specs=(vmem, vmem, vmem),
+        scratch_shapes=[
+            pltpu.VMEM((devices, 1, points), jnp.int32),
+            pltpu.SMEM((devices, 1, points), jnp.int32),
+            half_code,
+            half_code,
+            pltpu.SMEM((half, 1, points), jnp.int32),
+            pltpu.SMEM((clusters, entries), jnp.int32),
+            levels,
+            pltpu.VMEM((clusters, features, points), jnp.bfloat16),
+            levels,
+            half_tile, half_tile, half_tile, half_tile,
+            half_row, half_row, half_row, half_row,
+            row_block, row_block, row_block, row_block, row_block, row_block,
+            pltpu.VMEM((clusters, points, depth), jnp.bfloat16),
+            pltpu.VMEM((slots, depth, points), jnp.bfloat16),
+            kernel_block, kernel_block,
+            pltpu.VMEM((slots, points), jnp.float32),
+            levels, levels, levels,
+            pltpu.VMEM((clusters, 16, points), jnp.bfloat16),
+            pltpu.VMEM((slots, clusters * entries), jnp.float32),
+            pltpu.VMEM((clusters * entries, points), jnp.float32),
+            pltpu.SemaphoreType.DMA((2,)), sems, sems,
+        ],
+        compiler_params=pltpu.CompilerParams(
+            collective_id=8, has_side_effects=True, vmem_limit_bytes=60 * 1024 * 1024
+        ),
+        name="plan",
+    )(support, support, source, target, mass, target_mass, coarse)
+
+
+def careful(source_points, target_points, source_mass, target_mass, support, coarse_potential):
     devices = lax.axis_size(AXES)
     local_count, features, points = source_points.shape
     owner = support // local_count
@@ -300,7 +685,21 @@
                 turn_kernel, row_shape, [buffer, buffer], 2 + sweep, column, asked, target_mass
             )
     column_level = owner_call(finish_kernel, level_shape, [buffer], 1 + ITERS, column, asked)
-    return (source_sq - 0.5 * level, target_sq - 0.5 * column_level)
+    return level - 2.0 * source_sq, column_level - 2.0 * target_sq
+
+
+def body(source_points, target_points, source_mass, target_mass, support, coarse_potential):
+    f, g, flag = plan_call(
+        support, source_points, target_points, source_mass, target_mass, coarse_potential
+    )
+
+    def again():
+        return careful(
+            source_points, target_points, source_mass, target_mass, support, coarse_potential
+        )
+
+    f, g = lax.cond(flag[0, 0] > 0.0, again, lambda: (f, g))
+    return -0.5 * f, -0.5 * g
 
 
 def solution(mesh):

time: 127 us -> 70.4 us (0.55)
  Pallas kernels: 116 us -> 66.9 us
  other arithmetic: 4.63 us -> 0.61 us
  local copies, waits for them, and re-layouts: 4.74 us -> 1.23 us
    pallas_call x6 -> x1, Pallas kernels: 116 us -> 66.9 us  [plan_call(): pl.pallas_call(plan_kernel, out_shape=(level, level, jax.ShapeDtypeStruct...]
    reduce_sum x4 -> x0, other arithmetic: 1.93 us -> none  [the longest x2 1.1 us: squares(): return jnp.sum(wide * wide, axis=-2)]
    unnamed x16 -> x12, local copies, waits for them, and re-layouts: 1.9 us -> 0.03 us
    gather x1 -> x0, local copies, waits for them, and re-layouts: 1.71 us -> none  [body(): tiles, received = exchange([target_points[asked[:, :, 0]], sending], 1)]
    select_n x2 -> x0, other arithmetic: 1.33 us -> none  [the longest x1 0.71 us: body(): owner = support // local_count]
where the time goes in v2:
time: 70.4 us; the launch traced here: 70.3 us
  Pallas kernels  66.9 us (95%)
  between operations  1.4 us (2%)
  local copies, waits for them, and re-layouts  1.23 us (2%)
    pallas_call x1, Pallas kernels, plan_call(): pl.pallas_call(plan_kernel, out_shape=(level, level, jax.ShapeDtypeStruct...  66.9 us

profile of v2, /device:TPU:0, one launch (start us, length us, event | category | flops | bytes accessed | tf_op | source)
XLA Modules:
  0.0 70.3 jit_solution(444340202503933952)
XLA Ops:
  0.6 0.0 copy-start.1
  0.6 0.0 copy-start
  0.7 0.0 copy-start.4
  0.7 0.0 copy-start.5
  0.7 0.0 copy-start.6
  0.7 66.9 %plan.1 = (f32[16,128]{1,0:T(8,128)S(1)}, f32[16,128]{1,0:T(8,128)S(1)}, f32[8,128]{1,0:T(8,128)}) custom-call(s32[16,32]{1,0:T(8,128)} %names_ref.1, s32[16,32]{1,0:T(8,128)} %names_ref.1, bf16[16,64,128]{2,1,0:T(8,128)(2,1)} %source_ref.1, bf16[16,64,128]{2,1,0:T(8,128)(2,1)} %target_ref.1, f32[16,128]{1,0:T(8,128)} %mass_ref.1, ...), custom_call_target="tpu_custom_call" | custom-call | tf_op jit(solution)/shard_map/plan/pallas_call | solution.py:618
  67.5 0.0 copy-start.3
  67.6 1.2 %slice.6 = f32[1,1]{1,0:T(1,128)} slice(f32[8,128]{1,0:T(8,128)} %get-tuple-element.34), slice={[0:1], [0:1]} | slice | bytes 8 | tf_op jit(solution)/shard_map/slice | solution.py:701
  69.4 0.0 copy-done.1
  69.4 0.0 copy-done
  69.4 0.0 copy-done.4
  69.4 0.0 copy-done.5
  69.5 0.0 copy-done.6
  69.5 0.0 copy-done.3
  69.5 0.2 conditional.1
  69.7 0.6 broadcast_multiply_fusion
Async XLA Ops:
  0.6 68.8 %copy-start.1 = (bf16[16,64,128]{2,1,0:T(8,128)(2,1)S(1)}, bf16[16,64,128]{2,1,0:T(8,128)(2,1)}, u32[]{:S(2)}) copy-start(bf16[16,64,128]{2,1,0:T(8,128)(2,1)} %source_ref.1) | copy-start | bytes 786436
  0.6 68.8 %copy-start = (bf16[16,64,128]{2,1,0:T(8,128)(2,1)S(1)}, bf16[16,64,128]{2,1,0:T(8,128)(2,1)}, u32[]{:S(2)}) copy-start(bf16[16,64,128]{2,1,0:T(8,128)(2,1)} %target_ref.1) | copy-start | bytes 786436
  0.7 68.8 %copy-start.4 = (f32[16,128]{1,0:T(8,128)S(1)}, f32[16,128]{1,0:T(8,128)}, u32[]{:S(2)}) copy-start(f32[16,128]{1,0:T(8,128)} %target_mass_ref.1) | copy-start | bytes 24580
  0.7 68.8 %copy-start.5 = (f32[16,128]{1,0:T(8,128)S(1)}, f32[16,128]{1,0:T(8,128)}, u32[]{:S(2)}) copy-start(f32[16,128]{1,0:T(8,128)} %coarse_ref.1) | copy-start | bytes 24580
  0.7 68.8 %copy-start.6 = (f32[16,128]{1,0:T(8,128)S(1)}, f32[16,128]{1,0:T(8,128)}, u32[]{:S(2)}) copy-start(f32[16,128]{1,0:T(8,128)} %mass_ref.1) | copy-start | bytes 24580
  67.5 1.9 %copy-start.3 = (s32[16,32]{1,0:T(8,128)S(1)}, s32[16,32]{1,0:T(8,128)}, u32[]{:S(2)}) copy-start(s32[16,32]{1,0:T(8,128)} %names_ref.1) | copy-start | bytes 6148

commit v3 on v2

--- a/solution.py
+++ b/solution.py
@@ -12,7 +12,13 @@
 LIFT = 20.0
 FLOOR = 1e-10
 ALARM = 3e38
-SENDS = 10
+ROOM = 17 * 1024 * 1024
+TOGETHER = 2
+EARLY = 3
+CHUNKS = 2
+RELAY = 11
+PASS = RELAY + CHUNKS
+LOGICAL = pl.DeviceIdType.LOGICAL
 ITERS = 2
 AXES = ("row", "col")
 GROUP = 4
@@ -302,22 +308,25 @@
     return side, me - side * half, half, columns
 
 
-def block_of(step):
+def wrapped(value, size):
+    return value - jnp.where(value >= size, size, 0)
+
+
+def spot(other, step):
     side, mine, half, columns = halves()
-    other = lax.div(step, half)
-    near = lax.rem(mine + lax.rem(step, half), half)
-    device = lax.rem(side + other, 2) * half + near
-    return other * half + near, near, (lax.div(device, columns), lax.rem(device, columns))
-
-
-def start_copy(source, target, sems, index, where):
+    near = wrapped(mine + step, half)
+    base = (1 - side) * half if other else side * half
+    return near, base + near
+
+
+def start_copy(source, target, sems, index, where, arrival=None):
     pltpu.make_async_remote_copy(
         src_ref=source,
         dst_ref=target,
         send_sem=sems[0].at[index],
-        recv_sem=sems[1].at[index],
+        recv_sem=sems[1].at[index if arrival is None else arrival],
         device_id=where,
-        device_id_type=MESH,
+        device_id_type=LOGICAL,
     ).start()
 
 
@@ -327,28 +336,51 @@
 
 
 def plan_kernel(
-    support_ref, names_ref, source_ref, target_ref, mass_ref, target_mass_ref, coarse_ref,
+    support_in, source_in, target_in, mass_in, target_mass_in, coarse_in,
     f_ref, g_ref, flag_ref,
+    support_ref, names_ref, source_ref, target_ref, mass_ref, target_mass_ref, coarse_ref, input_sem,
     codes, codes_scalar, asked_near, asked_far, asked_scalar, slots_ref,
-    near, mate, mate_near, tile_out, mate_out, tiles, mate_tiles,
+    near, mate_near, tile_out, tiles,
     beta_out, mate_beta_out, betas, mate_betas, beta_next_out, beta_next,
     columns, parts, columns_next, parts_next,
-    left, right, store_even, store_odd, weight, sums, level_f, peaks, lifted, hot, rows,
-    local_sem, send_sem, recv_sem,
+    asked, requests, owners_of,
+    left, weight, sums, level_f, peaks, lifted, hot, rows,
+    local_sem, send_sem, recv_sem, near_sem, mate_sem, *more,
 ):
-    me, devices, _ = place()
+    _, devices, _ = place()
     side, mine, half, _ = halves()
+    inputs = (support_in, support_in, source_in, target_in, mass_in, target_mass_in, coarse_in)
+    landings = (support_ref, names_ref, source_ref, target_ref, mass_ref, target_mass_ref, coarse_ref)
     clusters, features, points = source_ref.shape
     entries = support_ref.shape[1]
     slots = devices * CAP
     sems = (send_sem, recv_sem)
+    mates, mate_outs, mate_tiles, stores = more[:CHUNKS], more[CHUNKS : 2 * CHUNKS], more[2 * CHUNKS : 3 * CHUNKS], more[3 * CHUNKS :]
+    roomy = len(stores) == 3
     barrier = pltpu.get_barrier_semaphore()
 
-    def signal(step, carry):
-        pl.semaphore_signal(barrier, inc=1, device_id=block_of(step)[2], device_id_type=MESH)
-        return carry
-
-    lax.fori_loop(1, devices, signal, 0, unroll=8)
+    def each_peer(use, between=None):
+        for other in range(2):
+            if other and between is not None:
+                between()
+
+            def one(step, carry):
+                use(other, *spot(other, step))
+                return carry
+
+            lax.fori_loop(1 - other, half, one, 0, unroll=8 if other else 5)
+
+    each_peer(
+        lambda other, near, where: pl.semaphore_signal(barrier, inc=1, device_id=where, device_id_type=LOGICAL)
+    )
+    loads = [
+        pltpu.make_async_copy(origin, landing, input_sem.at[index])
+        for index, (origin, landing) in enumerate(zip(inputs, landings))
+    ]
+    for load in loads:
+        load.start()
+    for load in loads:
+        load.wait()
 
     block = lax.broadcasted_iota(jnp.int32, (devices, entries), 0)
     far = jnp.where(block >= half, 1, 0)
@@ -377,21 +409,20 @@
     near[...] = 2.0 * coarse_ref[...] + target_mass_ref[...]
     pl.semaphore_wait(barrier, devices - 1)
 
-    def ask(step, carry):
-        to, _, where = block_of(step)
-        start_copy(codes.at[to], asked_near.at[mine], sems, 0, where)
-        return carry
-
-    def ask_far(step, carry):
-        to, _, where = block_of(step)
-        start_copy(codes.at[to], asked_far.at[mine], sems, 1, where)
-        return carry
-
-    lax.fori_loop(1, half, ask, 0, unroll=5)
-    mate_where = block_of(half)[2]
-    start_copy(target_ref, mate, sems, 2, mate_where)
-    start_copy(near, mate_near, sems, 3, mate_where)
-    lax.fori_loop(half, devices, ask_far, 0, unroll=8)
+    def ask(other, near_index, where):
+        start_copy(
+            codes.at[other * half + near_index], (asked_far if other else asked_near).at[mine], sems, other, where
+        )
+
+    chunk = features // CHUNKS
+
+    def relay():
+        where = spot(1, 0)[1]
+        start_copy(near, mate_near, sems, 3, where)
+        for index in range(CHUNKS):
+            start_copy(target_ref.at[:, pl.ds(index * chunk, chunk)], mates[index], sems, RELAY + index, where)
+
+    each_peer(ask, relay)
     local = pltpu.make_async_copy(codes, codes_scalar, local_sem.at[0])
     local.start()
 
@@ -399,9 +430,10 @@
         wide = source_ref[cluster].astype(jnp.float32)
         square = jnp.sum(wide * wide, axis=0, keepdims=True)
         stacked = jnp.concatenate([4.0 * wide, bias_rows(LIFT - 2.0 * square, False)], axis=0)
-        left[cluster] = stacked.T.astype(jnp.bfloat16)
+        left[pl.ds(cluster * points, points), :] = stacked.T.astype(jnp.bfloat16)
         return carry
 
+    lax.fori_loop(0, clusters, prepare_source, 0, unroll=2)
     local.wait()
     asked_near[mine] = codes[mine]
     wait_blocks(asked_near, half - 1, recv_sem.at[0])
@@ -409,27 +441,55 @@
     scalars.start()
     scalars.wait()
 
-    def serve(origin, origin_near, tile_to, beta_to, tile_in, beta_in, lane, index):
+    def picks(index, lane):
+        code = asked_scalar[index, 0, lane]
+        chosen = lax.div(code, clusters)
+        return enumerate((chosen, code - chosen * clusters))
+
+    def member(which, offset):
+        quarter = half // 2
+        group = lax.div(mine, quarter)
+        base = (1 - group) * quarter if which else group * quarter
+        return base + wrapped(mine - group * quarter + offset, quarter)
+
+    def serve(origin, outgoing, incoming, lane, index, arrival, shift):
+        for entry, pick in picks(mine, lane):
+            outgoing[mine, entry] = origin[pick]
+        pltpu.make_async_copy(outgoing.at[mine], incoming.at[mine], arrival.at[shift + mine]).start()
+        for which in (1, 0):
+
+            def one(step, carry):
+                near_index = member(which, step)
+                for entry, pick in picks(near_index, lane):
+                    outgoing[near_index, entry] = origin[pick]
+                start_copy(
+                    outgoing.at[near_index],
+                    incoming.at[mine],
+                    (send_sem, arrival),
+                    index,
+                    side * half + near_index,
+                    shift + mine,
+                )
+                return carry
+
+            lax.fori_loop(1 - which, half // 2, one, 0)
+
+    def serve_row(origin, outgoing, incoming, lane, index):
         def one(step, carry):
-            to, near_index, where = block_of(step)
-            code = asked_scalar[near_index, 0, lane]
-            chosen = lax.div(code, clusters)
-            for entry, pick in enumerate((chosen, code - chosen * clusters)):
-                tile_to[near_index, entry] = origin[pick]
-                beta_to[near_index, pl.ds(entry, 1), :] = origin_near[pl.ds(pick, 1), :]
-            start_copy(tile_to.at[near_index], tile_in.at[mine], sems, index, where)
-            start_copy(beta_to.at[near_index], beta_in.at[mine], sems, index + 1, where)
+            near_index, where = spot(0, step)
+            for entry, pick in picks(near_index, lane):
+                outgoing[near_index, pl.ds(entry, 1), :] = origin[pl.ds(pick, 1), :]
+            start_copy(outgoing.at[near_index], incoming.at[mine], sems, index, where)
             return carry
 
         lax.fori_loop(1, half, one, 0)
-        code = asked_scalar[mine, 0, lane]
-        chosen = lax.div(code, clusters)
-        for entry, pick in enumerate((chosen, code - chosen * clusters)):
-            tile_in[mine, entry] = origin[pick]
-            beta_in[mine, pl.ds(entry, 1), :] = origin_near[pl.ds(pick, 1), :]
-
-    serve(target_ref, near, tile_out, beta_out, tiles, betas, 0, 4)
-    lax.fori_loop(0, clusters, prepare_source, 0, unroll=2)
+        for entry, pick in picks(mine, lane):
+            incoming[mine, pl.ds(entry, 1), :] = origin[pl.ds(pick, 1), :]
+
+    wait_blocks(mate_near, None, recv_sem.at[3])
+    serve_row(near, beta_out, betas, 0, 5)
+    serve_row(mate_near, mate_beta_out, mate_betas, points // 2, 7)
+    serve(target_ref, tile_out, tiles, 0, 4, near_sem, 0)
 
     def place_slots(cluster, carry):
         for entry in range(entries):
@@ -446,43 +506,147 @@
         hot[:, cluster * entries : (cluster + 1) * entries] = jnp.where(
             names_ref[cluster : cluster + 1, :] == slot_name, 1.0, 0.0
         )
-    wait_blocks(mate, None, recv_sem.at[2])
-    wait_blocks(mate_near, None, recv_sem.at[3])
-    serve(mate, mate_near, mate_out, mate_beta_out, mate_tiles, mate_betas, points // 2, 6)
-
-    def prepare_target(source, offset):
-        def one(owner, carry):
-            for entry in range(CAP):
-                tile = source[owner, entry]
-                wide = tile.astype(jnp.float32)
-                square = jnp.sum(wide * wide, axis=0, keepdims=True)
-                extra = bias_rows(LIFT - 2.0 * square, True).astype(jnp.bfloat16)
-                right[offset + owner * CAP + entry] = jnp.concatenate([tile, extra], axis=0)
-            return carry
-
-        lax.fori_loop(0, half, one, 0, unroll=4)
-
-    wait_blocks(betas, half - 1, recv_sem.at[5])
-    wait_blocks(tiles, half - 1, recv_sem.at[4])
-    prepare_target(tiles, 0)
-    wait_blocks(mate_betas, half - 1, recv_sem.at[7])
-    wait_blocks(mate_tiles, half - 1, recv_sem.at[6])
-    prepare_target(mate_tiles, half * CAP)
-    wait_blocks(asked_far, half, recv_sem.at[1])
-    asked_own = jnp.concatenate([asked_near[...], asked_far[...]], axis=0)[:, :, 0:1]
-    asked_code = jnp.broadcast_to(asked_own, (devices, CAP, points))
-    asked_first = lax.div(asked_code, clusters)
-    asked = jnp.where(
-        lax.broadcasted_iota(jnp.int32, (devices, CAP, points), 1) == 0,
-        asked_first,
-        asked_code - asked_first * clusters,
-    )
-
     def set_weights(values):
         top = whole_max(values)
         weight[...] = jnp.exp(values - top)
         return top
 
+    def joined(sources, owner, entry):
+        return jnp.concatenate([source[owner, entry] for source in sources], axis=0)
+
+    def augmented(tile):
+        wide = tile.astype(jnp.float32)
+        square = jnp.sum(wide * wide, axis=0, keepdims=True)
+        extra = bias_rows(LIFT - 2.0 * square, True).astype(jnp.bfloat16)
+        return jnp.concatenate([tile, extra], axis=0)
+
+    def arrivals(sources, arrival, use, begin, end):
+        for which in range(2):
+
+            def one(step, carry):
+                owners = []
+                for lane in range(TOGETHER):
+                    owner = member(which, half // 2 - (step * TOGETHER + lane))
+                    for index, source in enumerate(sources):
+                        wait_blocks(source.at[owner], None, arrival.at[index * half + owner])
+                    owners.append(owner)
+                use(owners)
+                return carry
+
+            steps = half // 2 // TOGETHER
+            lax.fori_loop(
+                max(begin - which * steps, 0), max(min(end - which * steps, steps), 0), one, 0
+            )
+
+    def serve_mates(index):
+        wait_blocks(mates[index], None, recv_sem.at[RELAY + index])
+        serve(
+            mates[index], mate_outs[index], mate_tiles[index], points // 2, PASS + index, mate_sem, index * half
+        )
+
+    def set_asked():
+        wait_blocks(asked_far, half, recv_sem.at[1])
+        asked_own = jnp.concatenate([asked_near[...], asked_far[...]], axis=0)[:, :, 0:1]
+        asked_code = jnp.broadcast_to(asked_own, (devices, CAP, points))
+        asked_first = lax.div(asked_code, clusters)
+        picked = jnp.where(
+            lax.broadcasted_iota(jnp.int32, (devices, CAP, points), 1) == 0,
+            asked_first,
+            asked_code - asked_first * clusters,
+        ).reshape(slots, points)
+        asked[...] = picked
+        matrix = jnp.where(picked == lax.broadcasted_iota(jnp.int32, (slots, points), 1), 1.0, 0.0)
+        requests[...] = matrix.astype(jnp.bfloat16)
+        owners_of[...] = matrix.T[:clusters].astype(jnp.bfloat16)
+
+    def spread(values, count):
+        padded = jnp.concatenate([values, jnp.zeros((points - clusters, points), jnp.float32)], axis=0)
+        total = jnp.zeros((slots, points), jnp.float32)
+        for _ in range(count):
+            piece = padded.astype(jnp.bfloat16)
+            total = total + jnp.dot(requests[...], piece, preferred_element_type=jnp.float32)
+            padded = padded - piece.astype(jnp.float32)
+        return total
+
+    def owned_levels(parts_ref):
+        values = parts_ref[...].reshape(slots, points)
+        names = asked[...]
+        peak = jnp.concatenate(
+            [
+                jnp.max(jnp.where(names == cluster, values, lowest), axis=0, keepdims=True)
+                for cluster in range(clusters)
+            ],
+            axis=0,
+        )
+        peak = peak.astype(jnp.bfloat16).astype(jnp.float32)
+        shares = jnp.exp(values - spread(peak, 1))
+        total = jnp.zeros((clusters, points), jnp.float32)
+        for _ in range(2):
+            piece = shares.astype(jnp.bfloat16)
+            total = total + jnp.dot(owners_of[...], piece, preferred_element_type=jnp.float32)
+            shares = shares - piece.astype(jnp.float32)
+        return peak + jnp.log(total)
+
+    groups = half // TOGETHER
+    early = groups * EARLY // 8
+    for index in range(CHUNKS - 1):
+        serve_mates(index)
+    wait_blocks(betas, half - 1, recv_sem.at[5])
+    wait_blocks(mate_betas, half - 1, recv_sem.at[7])
+    start = jnp.concatenate([betas[...], mate_betas[...]], axis=0).reshape(slots, points)
+    start_top = set_weights(start)
+
+    if roomy:
+        store, gathered, total_store = stores
+        span = clusters // 4
+        for cluster in range(clusters):
+            count = jnp.sum(hot[:, cluster * entries : (cluster + 1) * entries], axis=1, keepdims=True)
+            gathered[cluster] = weight[...] * count
+        total_store[...] = jnp.zeros(total_store.shape, jnp.float32)
+
+        def use_tile(sources, offset):
+            def use(owners):
+                picked = [(owner, entry) for owner in owners for entry in range(CAP)]
+                rhs = jnp.concatenate([augmented(joined(sources, owner, entry)) for owner, entry in picked], axis=1)
+                for part in range(4):
+                    first_row = part * span * points
+                    values = jnp.exp(
+                        jnp.dot(
+                            left[first_row : first_row + span * points, :], rhs, preferred_element_type=jnp.float32
+                        )
+                    )
+                    for lane, (owner, entry) in enumerate(picked):
+                        slot = (offset + owner) * CAP + entry
+                        store[slot, first_row : first_row + span * points, :] = values[
+                            :, lane * points : (lane + 1) * points
+                        ].astype(jnp.bfloat16)
+                    for index in range(span):
+                        cluster = part * span + index
+                        added = 0.0
+                        for lane, (owner, entry) in enumerate(picked):
+                            block = values[index * points : (index + 1) * points, lane * points : (lane + 1) * points]
+                            slot = (offset + owner) * CAP + entry
+                            added = added + block * gathered[cluster, pl.ds(slot, 1), :]
+                        total_store[cluster] += added
+
+            return use
+
+    else:
+        right, store_even, store_odd = stores[:3]
+
+        def use_tile(sources, offset):
+            def use(owners):
+                for owner in owners:
+                    for entry in range(CAP):
+                        right[(offset + owner) * CAP + entry] = augmented(joined(sources, owner, entry))
+
+            return use
+
+    arrivals([tiles], near_sem, use_tile([tiles], 0), 0, early)
+    serve_mates(CHUNKS - 1)
+    arrivals([tiles], near_sem, use_tile([tiles], 0), early, groups)
+    set_asked()
+    arrivals(mate_tiles, mate_sem, use_tile(mate_tiles, half), 0, groups)
     def close(cluster, total, top):
         row = jnp.sum(total.T, axis=0, keepdims=True)
         level = jnp.log(row) + (top - 2.0 * LIFT)
@@ -493,53 +657,86 @@
         peaks[pl.ds(cluster, 1), :] = jnp.broadcast_to(peak, (1, points))
         lifted[cluster] = split_rows(jnp.exp(alpha - peak))
 
-    def build(cluster, store, index, pair, total):
+    def blocks(cluster, held, pair):
+        if roomy:
+            return [
+                held[0][slots_ref[cluster, 2 * pair + lane], pl.ds(cluster * points, points), :] for lane in range(2)
+            ]
+        pairs = held[0][held[1], :, pl.ds(pair * 2 * points, 2 * points)]
+        return [pairs[:, lane * points : (lane + 1) * points] for lane in range(2)]
+
+    def build(cluster, held, pair, total):
         chosen = [slots_ref[cluster, 2 * pair + lane] for lane in range(2)]
         rhs = jnp.concatenate([right[slot] for slot in chosen], axis=1)
-        values = jnp.exp(jnp.dot(left[cluster], rhs, preferred_element_type=jnp.float32))
-        store[index, :, pl.ds(pair * 2 * points, 2 * points)] = values.astype(jnp.bfloat16)
+        values = jnp.exp(
+            jnp.dot(left[pl.ds(cluster * points, points), :], rhs, preferred_element_type=jnp.float32)
+        )
+        held[0][held[1], :, pl.ds(pair * 2 * points, 2 * points)] = values.astype(jnp.bfloat16)
         for lane, slot in enumerate(chosen):
             total = total + values[:, lane * points : (lane + 1) * points] * weight[pl.ds(slot, 1), :]
         return total
 
-    def forward(cluster, store, index, pair, total):
-        for lane in range(2):
-            entry = 2 * pair + lane
-            values = store[index, :, pl.ds(entry * points, points)].astype(jnp.float32)
-            total = total + values * weight[pl.ds(slots_ref[cluster, entry], 1), :]
+    def forward(cluster, held, pair, total):
+        for lane, values in enumerate(blocks(cluster, held, pair)):
+            slot = slots_ref[cluster, 2 * pair + lane]
+            total = total + values.astype(jnp.float32) * weight[pl.ds(slot, 1), :]
         return total
 
-    def backward(cluster, store, index, pair):
+    def backward(cluster, held, pair):
         products = jnp.dot(
             lifted[cluster],
-            store[index, :, pl.ds(pair * 2 * points, 2 * points)],
+            jnp.concatenate(blocks(cluster, held, pair), axis=1),
             preferred_element_type=jnp.float32,
         )
         row = products[0:1] + products[1:2]
         for lane in range(2):
             rows[pl.ds(cluster * entries + 2 * pair + lane, 1), :] = row[:, lane * points : (lane + 1) * points]
 
+    def even(index):
+        return (store,) if roomy else (store_even, index)
+
+    def odd(index):
+        return (store,) if roomy else (store_odd, index)
+
     def sweep(make, top):
-        def mixed(cluster, store, index, before, old_store, old_index):
+        def mixed(cluster, held, before, held_before):
             total = jnp.zeros((points, points), jnp.float32)
             for pair in range(entries // 2):
                 if before is not None:
-                    backward(before, old_store, old_index, pair)
+                    backward(before, held_before, pair)
                 if cluster is not None:
-                    total = make(cluster, store, index, pair, total)
+                    total = make(cluster, held, pair, total)
             if cluster is not None:
                 close(cluster, total, top)
 
         def both(index, carry):
-            mixed(2 * index + 1, store_odd, index, 2 * index, store_even, index)
-            mixed(2 * index + 2, store_even, index + 1, 2 * index + 1, store_odd, index)
+            mixed(2 * index + 1, odd(index), 2 * index, even(index))
+            mixed(2 * index + 2, even(index + 1), 2 * index + 1, odd(index))
             return carry
 
         last = clusters // 2 - 1
-        mixed(0, store_even, 0, None, None, None)
+        mixed(0, even(0), None, None)
         lax.fori_loop(0, last, both, 0)
-        mixed(clusters - 1, store_odd, last, clusters - 2, store_even, last)
-        mixed(None, None, None, clusters - 1, store_odd, last)
+        mixed(clusters - 1, odd(last), clusters - 2, even(last))
+        mixed(None, None, clusters - 1, odd(last))
+        return finish()
+
+    def first_sweep(top):
+        def closing(cluster, carry):
+            close(cluster, total_store[cluster], top)
+            return carry
+
+        def returning(index, carry):
+            for lane in range(2):
+                for pair in range(entries // 2):
+                    backward(2 * index + lane, (store,), pair)
+            return carry
+
+        lax.fori_loop(0, clusters, closing, 0, unroll=4)
+        lax.fori_loop(0, clusters // 2, returning, 0)
+        return finish()
+
+    def finish():
         peak = whole_max(peaks[...])
         scale = jnp.exp(peaks[...] - peak)
         total = jnp.zeros((slots, points), jnp.float32)
@@ -551,7 +748,7 @@
             axis=0,
         )
         choice = hot[...].astype(jnp.bfloat16)
-        for _ in range(3):
+        for _ in range(2):
             piece = values.astype(jnp.bfloat16)
             total = total + jnp.dot(choice, piece, preferred_element_type=jnp.float32)
             values = values - piece.astype(jnp.float32)
@@ -562,37 +759,32 @@
         return jnp.where(low > 0.0, ALARM, column).reshape(devices, CAP, points)
 
     def return_columns(source, target, index):
-        def one(step, carry):
-            to, near_index, where = block_of(step)
-            landing = lax.div(to, half) * half + mine
-            start_copy(source.at[to], target.at[landing], sems, index, where)
-            return carry
-
-        lax.fori_loop(1, devices, one, 0, unroll=8)
+        each_peer(
+            lambda other, near_index, where: start_copy(
+                source.at[other * half + near_index], target.at[other * half + mine], sems, index, where
+            )
+        )
         target[mine] = source[mine]
         wait_blocks(target, devices - 1, recv_sem.at[index])
 
-    start = jnp.concatenate([betas[...], mate_betas[...]], axis=0).reshape(slots, points)
-    columns[...] = sweep(build, set_weights(start))
+    columns[...] = first_sweep(start_top) if roomy else sweep(build, start_top)
     return_columns(columns, parts, 8)
-    for cluster in range(clusters):
-        near_row = target_mass_ref[cluster : cluster + 1, :] - combined(asked, parts[...], cluster)
-        beta_next_out[...] = jnp.where(asked == cluster, near_row[None], beta_next_out[...] if cluster else 0.0)
+    beta_next_out[...] = spread(target_mass_ref[...] - owned_levels(parts), 3).reshape(devices, CAP, points)
     return_columns(beta_next_out, beta_next, 9)
     columns_next[...] = sweep(forward, set_weights(beta_next[...].reshape(slots, points)))
     f_ref[...] = level_f[...]
     return_columns(columns_next, parts_next, 10)
-    for cluster in range(clusters):
-        g_ref[cluster : cluster + 1, :] = combined(asked, parts_next[...], cluster)
+    g_ref[...] = owned_levels(parts_next)
     alarm = jnp.maximum(parts[...].reshape(slots, points), parts_next[...].reshape(slots, points))
-    flag_ref[...] = jnp.broadcast_to(whole_max(jnp.where(alarm < 1e30, 0.0, 1.0)), flag_ref.shape)
+    flag_ref[0, 0] = jnp.max(jnp.where(alarm < 1e30, 0.0, 1.0)).astype(jnp.int32)
     wait_blocks(codes, half - 1, send_sem.at[0])
     wait_blocks(codes, half, send_sem.at[1])
-    wait_blocks(mate, None, send_sem.at[2])
+    for index in range(CHUNKS):
+        wait_blocks(mates[index], None, send_sem.at[RELAY + index])
+        wait_blocks(mate_outs[index], half - 1, send_sem.at[PASS + index])
     wait_blocks(near, None, send_sem.at[3])
     wait_blocks(tile_out, half - 1, send_sem.at[4])
     wait_blocks(beta_out, half - 1, send_sem.at[5])
-    wait_blocks(mate_out, half - 1, send_sem.at[6])
     wait_blocks(mate_beta_out, half - 1, send_sem.at[7])
     wait_blocks(columns, devices - 1, send_sem.at[8])
     wait_blocks(beta_next_out, devices - 1, send_sem.at[9])
@@ -612,15 +804,31 @@
     row_block = pltpu.VMEM((devices, CAP, points), jnp.float32)
     half_row = pltpu.VMEM((half, CAP, points), jnp.float32)
     half_tile = pltpu.VMEM((half, CAP, features, points), jnp.bfloat16)
+    whole_tile = pltpu.VMEM((clusters, features, points), jnp.bfloat16)
     half_code = pltpu.VMEM((half, 1, points), jnp.int32)
-    kernel_block = pltpu.VMEM((clusters // 2, points, entries * points), jnp.bfloat16)
-    sems = pltpu.SemaphoreType.DMA((11,))
+    roomy = slots * clusters * points * points <= ROOM
+    if roomy:
+        stores = [
+            pltpu.VMEM((slots, clusters * points, points), jnp.bfloat16),
+            pltpu.VMEM((clusters, slots, points), jnp.float32),
+            pltpu.VMEM((clusters, points, points), jnp.float32),
+        ]
+    else:
+        kernel_block = pltpu.VMEM((clusters // 2, points, entries * points), jnp.bfloat16)
+        stores = [pltpu.VMEM((slots, depth, points), jnp.bfloat16), kernel_block, kernel_block, pltpu.SMEM((1,), jnp.int32)]
+    sems = pltpu.SemaphoreType.DMA((PASS + CHUNKS,))
     return pl.pallas_call(
         plan_kernel,
-        out_shape=(level, level, jax.ShapeDtypeStruct((8, points), jnp.float32)),
-        in_specs=[pl.BlockSpec(memory_space=pltpu.SMEM)] + [vmem] * 6,
-        out_specs=(vmem, vmem, vmem),
+        out_shape=(level, level, jax.ShapeDtypeStruct((1, 1), jnp.int32)),
+        in_specs=[pl.BlockSpec(memory_space=pltpu.HBM)] * 6,
+        out_specs=(vmem, vmem, pl.BlockSpec(memory_space=pltpu.SMEM)),
         scratch_shapes=[
+            pltpu.SMEM((clusters, entries), jnp.int32),
+            pltpu.VMEM((clusters, entries), jnp.int32),
+            whole_tile,
+            whole_tile,
+            levels, levels, levels,
+            pltpu.SemaphoreType.DMA((7,)),
             pltpu.VMEM((devices, 1, points), jnp.int32),
             pltpu.SMEM((devices, 1, points), jnp.int32),
             half_code,
@@ -628,26 +836,30 @@
             pltpu.SMEM((half, 1, points), jnp.int32),
             pltpu.SMEM((clusters, entries), jnp.int32),
             levels,
-            pltpu.VMEM((clusters, features, points), jnp.bfloat16),
             levels,
-            half_tile, half_tile, half_tile, half_tile,
+            half_tile, half_tile,
             half_row, half_row, half_row, half_row,
             row_block, row_block, row_block, row_block, row_block, row_block,
-            pltpu.VMEM((clusters, points, depth), jnp.bfloat16),
-            pltpu.VMEM((slots, depth, points), jnp.bfloat16),
-            kernel_block, kernel_block,
+            pltpu.VMEM((slots, points), jnp.int32),
+            pltpu.VMEM((slots, points), jnp.bfloat16),
+            pltpu.VMEM((clusters, slots), jnp.bfloat16),
+            pltpu.VMEM((clusters * points, depth), jnp.bfloat16),
             pltpu.VMEM((slots, points), jnp.float32),
             levels, levels, levels,
             pltpu.VMEM((clusters, 16, points), jnp.bfloat16),
             pltpu.VMEM((slots, clusters * entries), jnp.float32),
             pltpu.VMEM((clusters * entries, points), jnp.float32),
             pltpu.SemaphoreType.DMA((2,)), sems, sems,
-        ],
+            pltpu.SemaphoreType.DMA((half,)), pltpu.SemaphoreType.DMA((CHUNKS * half,)),
+        ]
+        + [pltpu.VMEM((clusters, features // CHUNKS, points), jnp.bfloat16)] * CHUNKS
+        + [pltpu.VMEM((half, CAP, features // CHUNKS, points), jnp.bfloat16)] * (2 * CHUNKS)
+        + stores,
         compiler_params=pltpu.CompilerParams(
             collective_id=8, has_side_effects=True, vmem_limit_bytes=60 * 1024 * 1024
         ),
         name="plan",
-    )(support, support, source, target, mass, target_mass, coarse)
+    )(support, source, target, mass, target_mass, coarse)
 
 
 def careful(source_points, target_points, source_mass, target_mass, support, coarse_potential):
@@ -698,7 +910,7 @@
             source_points, target_points, source_mass, target_mass, support, coarse_potential
         )
 
-    f, g = lax.cond(flag[0, 0] > 0.0, again, lambda: (f, g))
+    f, g = lax.cond(flag[0, 0] > 0, again, lambda: (f, g))
     return -0.5 * f, -0.5 * g
 
 

time: 70.4 us -> 66.7 us (0.947)
  Pallas kernels: 66.9 us -> 64.2 us
  local copies, waits for them, and re-layouts: 1.23 us -> 0.03 us
    pallas_call x1, Pallas kernels: 66.9 us -> 64.2 us  [plan_call(): pl.pallas_call(plan_kernel, out_shape=(level, level, jax.ShapeDtypeStruct...]
    slice x1 -> x0, local copies, waits for them, and re-layouts: 1.2 us -> none  [body(): f, g = lax.cond(flag[0, 0] > 0.0, again, lambda: (f, g))]
where the time goes in v3:
time: 66.7 us; the launch traced here: 66.5 us
  Pallas kernels  64.2 us (96%)
  between operations  1.45 us (2%)
    pallas_call x1, Pallas kernels, plan_call(): pl.pallas_call(plan_kernel, out_shape=(level, level, jax.ShapeDtypeStruct...  64.2 us

profile of v3, /device:TPU:0, one launch (start us, length us, event | category | flops | bytes accessed | tf_op | source)
XLA Modules:
  0.0 66.5 jit_solution(12142324299832795937)
XLA Ops:
  0.6 0.0 copy-start.1
  0.6 0.0 copy-start
  0.7 0.0 copy-start.4
  0.7 0.0 copy-start.5
  0.7 0.0 copy-start.6
  0.7 64.2 %plan.1 = (f32[16,128]{1,0:T(8,128)S(1)}, f32[16,128]{1,0:T(8,128)S(1)}, s32[1,1]{1,0:T(1,128)}) custom-call(s32[16,32]{1,0:T(8,128)} %support_in.1, bf16[16,64,128]{2,1,0:T(8,128)(2,1)} %source_in.1, bf16[16,64,128]{2,1,0:T(8,128)(2,1)} %target_in.1, f32[16,128]{1,0:T(8,128)} %mass_in.1, f32[16,128]{1,0:T(8,128)} %target_mass_in.1, f32[16,128]{1,0:T(8,128)} %coarse_in.1), custom_call_target="tpu_custom_call" | custom-call | tf_op jit(solution)/shard_map/plan/pallas_call | solution.py:820
  64.9 0.0 copy-start.3
  65.7 0.0 copy-done.1
  65.7 0.0 copy-done
  65.7 0.0 copy-done.4
  65.7 0.0 copy-done.5
  65.7 0.0 copy-done.6
  65.7 0.0 copy-done.3
  65.7 0.2 conditional.1
  65.9 0.6 broadcast_multiply_fusion
Async XLA Ops:
  0.6 65.0 %copy-start.1 = (bf16[16,64,128]{2,1,0:T(8,128)(2,1)S(1)}, bf16[16,64,128]{2,1,0:T(8,128)(2,1)}, u32[]{:S(2)}) copy-start(bf16[16,64,128]{2,1,0:T(8,128)(2,1)} %source_in.1) | copy-start | bytes 786436
  0.6 65.0 %copy-start = (bf16[16,64,128]{2,1,0:T(8,128)(2,1)S(1)}, bf16[16,64,128]{2,1,0:T(8,128)(2,1)}, u32[]{:S(2)}) copy-start(bf16[16,64,128]{2,1,0:T(8,128)(2,1)} %target_in.1) | copy-start | bytes 786436
  0.7 65.0 %copy-start.4 = (f32[16,128]{1,0:T(8,128)S(1)}, f32[16,128]{1,0:T(8,128)}, u32[]{:S(2)}) copy-start(f32[16,128]{1,0:T(8,128)} %target_mass_in.1) | copy-start | bytes 24580
  0.7 65.0 %copy-start.5 = (f32[16,128]{1,0:T(8,128)S(1)}, f32[16,128]{1,0:T(8,128)}, u32[]{:S(2)}) copy-start(f32[16,128]{1,0:T(8,128)} %coarse_in.1) | copy-start | bytes 24580
  0.7 65.0 %copy-start.6 = (f32[16,128]{1,0:T(8,128)S(1)}, f32[16,128]{1,0:T(8,128)}, u32[]{:S(2)}) copy-start(f32[16,128]{1,0:T(8,128)} %mass_in.1) | copy-start | bytes 24580
  64.9 0.8 %copy-start.3 = (s32[16,32]{1,0:T(8,128)S(1)}, s32[16,32]{1,0:T(8,128)}, u32[]{:S(2)}) copy-start(s32[16,32]{1,0:T(8,128)} %support_in.1) | copy-start | bytes 6148

commit v4 on v3

--- a/solution.py
+++ b/solution.py
@@ -15,7 +15,8 @@
 ROOM = 17 * 1024 * 1024
 TOGETHER = 2
 EARLY = 3
-CHUNKS = 2
+CHUNKS = 1
+PARTS = 4
 RELAY = 11
 PASS = RELAY + CHUNKS
 LOGICAL = pl.DeviceIdType.LOGICAL
@@ -456,7 +457,7 @@
         for entry, pick in picks(mine, lane):
             outgoing[mine, entry] = origin[pick]
         pltpu.make_async_copy(outgoing.at[mine], incoming.at[mine], arrival.at[shift + mine]).start()
-        for which in (1, 0):
+        for which in (0, 1):
 
             def one(step, carry):
                 near_index = member(which, step)
@@ -472,7 +473,7 @@
                 )
                 return carry
 
-            lax.fori_loop(1 - which, half // 2, one, 0)
+            lax.fori_loop(1 - which, half // 2, one, 0, unroll=4 if which else half // 2 - 1)
 
     def serve_row(origin, outgoing, incoming, lane, index):
         def one(step, carry):
@@ -482,7 +483,7 @@
             start_copy(outgoing.at[near_index], incoming.at[mine], sems, index, where)
             return carry
 
-        lax.fori_loop(1, half, one, 0)
+        lax.fori_loop(1, half, one, 0, unroll=5)
         for entry, pick in picks(mine, lane):
             incoming[mine, pl.ds(entry, 1), :] = origin[pl.ds(pick, 1), :]
 
@@ -700,14 +701,17 @@
 
     def sweep(make, top):
         def mixed(cluster, held, before, held_before):
-            total = jnp.zeros((points, points), jnp.float32)
-            for pair in range(entries // 2):
-                if before is not None:
-                    backward(before, held_before, pair)
-                if cluster is not None:
-                    total = make(cluster, held, pair, total)
+            total = None if cluster is None else total_store[cluster] if make is None else jnp.zeros((points, points), jnp.float32)
+            done = []
+            pairs = entries // 2
+            for part in range(PARTS):
+                for pair in range(part * pairs // PARTS, (part + 1) * pairs // PARTS):
+                    if before is not None:
+                        backward(before, held_before, pair)
+                    if make is not None and cluster is not None:
+                        total = make(cluster, held, pair, total)
             if cluster is not None:
-                close(cluster, total, top)
+                close(cluster, jnp.concatenate(done, axis=0) if done else total, top)
 
         def both(index, carry):
             mixed(2 * index + 1, odd(index), 2 * index, even(index))
@@ -719,21 +723,6 @@
         lax.fori_loop(0, last, both, 0)
         mixed(clusters - 1, odd(last), clusters - 2, even(last))
         mixed(None, None, clusters - 1, odd(last))
-        return finish()
-
-    def first_sweep(top):
-        def closing(cluster, carry):
-            close(cluster, total_store[cluster], top)
-            return carry
-
-        def returning(index, carry):
-            for lane in range(2):
-                for pair in range(entries // 2):
-                    backward(2 * index + lane, (store,), pair)
-            return carry
-
-        lax.fori_loop(0, clusters, closing, 0, unroll=4)
-        lax.fori_loop(0, clusters // 2, returning, 0)
         return finish()
 
     def finish():
@@ -767,7 +756,7 @@
         target[mine] = source[mine]
         wait_blocks(target, devices - 1, recv_sem.at[index])
 
-    columns[...] = first_sweep(start_top) if roomy else sweep(build, start_top)
+    columns[...] = sweep(None if roomy else build, start_top)
     return_columns(columns, parts, 8)
     beta_next_out[...] = spread(target_mass_ref[...] - owned_levels(parts), 3).reshape(devices, CAP, points)
     return_columns(beta_next_out, beta_next, 9)

time: 66.7 us -> 65.1 us (0.976)
  Pallas kernels: 64.2 us -> 62.6 us
    pallas_call x1, Pallas kernels: 64.2 us -> 62.6 us  [plan_call(): pl.pallas_call(plan_kernel, out_shape=(level, level, jax.ShapeDtypeStruct...]
where the time goes in v4:
time: 65.1 us; the launch traced here: 64.9 us
  Pallas kernels  62.6 us (96%)
  between operations  1.45 us (2%)
    pallas_call x1, Pallas kernels, plan_call(): pl.pallas_call(plan_kernel, out_shape=(level, level, jax.ShapeDtypeStruct...  62.6 us

profile of v4, /device:TPU:0, one launch (start us, length us, event | category | flops | bytes accessed | tf_op | source)
XLA Modules:
  0.0 64.9 jit_solution(18123930494670877430)
XLA Ops:
  0.6 0.0 copy-start.1
  0.6 0.0 copy-start
  0.7 0.0 copy-start.4
  0.7 0.0 copy-start.5
  0.7 0.0 copy-start.6
  0.7 62.6 %plan.1 = (f32[16,128]{1,0:T(8,128)S(1)}, f32[16,128]{1,0:T(8,128)S(1)}, s32[1,1]{1,0:T(1,128)}) custom-call(s32[16,32]{1,0:T(8,128)} %support_in.1, bf16[16,64,128]{2,1,0:T(8,128)(2,1)} %source_in.1, bf16[16,64,128]{2,1,0:T(8,128)(2,1)} %target_in.1, f32[16,128]{1,0:T(8,128)} %mass_in.1, f32[16,128]{1,0:T(8,128)} %target_mass_in.1, f32[16,128]{1,0:T(8,128)} %coarse_in.1), custom_call_target="tpu_custom_call" | custom-call | tf_op jit(solution)/shard_map/plan/pallas_call | solution.py:809
  63.3 0.0 copy-start.3
  64.0 0.0 copy-done.1
  64.0 0.0 copy-done
  64.1 0.0 copy-done.4
  64.1 0.0 copy-done.5
  64.1 0.0 copy-done.6
  64.1 0.0 copy-done.3
  64.1 0.2 conditional.1
  64.3 0.6 broadcast_multiply_fusion
Async XLA Ops:
  0.6 63.4 %copy-start.1 = (bf16[16,64,128]{2,1,0:T(8,128)(2,1)S(1)}, bf16[16,64,128]{2,1,0:T(8,128)(2,1)}, u32[]{:S(2)}) copy-start(bf16[16,64,128]{2,1,0:T(8,128)(2,1)} %source_in.1) | copy-start | bytes 786436
  0.6 63.4 %copy-start = (bf16[16,64,128]{2,1,0:T(8,128)(2,1)S(1)}, bf16[16,64,128]{2,1,0:T(8,128)(2,1)}, u32[]{:S(2)}) copy-start(bf16[16,64,128]{2,1,0:T(8,128)(2,1)} %target_in.1) | copy-start | bytes 786436
  0.7 63.4 %copy-start.4 = (f32[16,128]{1,0:T(8,128)S(1)}, f32[16,128]{1,0:T(8,128)}, u32[]{:S(2)}) copy-start(f32[16,128]{1,0:T(8,128)} %target_mass_in.1) | copy-start | bytes 24580
  0.7 63.4 %copy-start.5 = (f32[16,128]{1,0:T(8,128)S(1)}, f32[16,128]{1,0:T(8,128)}, u32[]{:S(2)}) copy-start(f32[16,128]{1,0:T(8,128)} %coarse_in.1) | copy-start | bytes 24580
  0.7 63.4 %copy-start.6 = (f32[16,128]{1,0:T(8,128)S(1)}, f32[16,128]{1,0:T(8,128)}, u32[]{:S(2)}) copy-start(f32[16,128]{1,0:T(8,128)} %mass_in.1) | copy-start | bytes 24580
  63.3 0.8 %copy-start.3 = (s32[16,32]{1,0:T(8,128)S(1)}, s32[16,32]{1,0:T(8,128)}, u32[]{:S(2)}) copy-start(s32[16,32]{1,0:T(8,128)} %support_in.1) | copy-start | bytes 6148

commit v5 on v4

--- a/solution.py
+++ b/solution.py
@@ -13,7 +13,7 @@
 FLOOR = 1e-10
 ALARM = 3e38
 ROOM = 17 * 1024 * 1024
-TOGETHER = 2
+TOGETHER = 4
 EARLY = 3
 CHUNKS = 1
 PARTS = 4
@@ -599,7 +599,7 @@
 
     if roomy:
         store, gathered, total_store = stores
-        span = clusters // 4
+        span = clusters // 2
         for cluster in range(clusters):
             count = jnp.sum(hot[:, cluster * entries : (cluster + 1) * entries], axis=1, keepdims=True)
             gathered[cluster] = weight[...] * count
@@ -609,7 +609,7 @@
             def use(owners):
                 picked = [(owner, entry) for owner in owners for entry in range(CAP)]
                 rhs = jnp.concatenate([augmented(joined(sources, owner, entry)) for owner, entry in picked], axis=1)
-                for part in range(4):
+                for part in range(2):
                     first_row = part * span * points
                     values = jnp.exp(
                         jnp.dot(

time: 65.1 us -> 64.1 us (0.985)
  Pallas kernels: 62.6 us -> 61.8 us
    pallas_call x1, Pallas kernels: 62.6 us -> 61.8 us  [plan_call(): pl.pallas_call(plan_kernel, out_shape=(level, level, jax.ShapeDtypeStruct...]
where the time goes in v5:
time: 64.1 us; the launch traced here: 63.9 us
  Pallas kernels  61.8 us (96%)
  between operations  1.45 us (2%)
    pallas_call x1, Pallas kernels, plan_call(): pl.pallas_call(plan_kernel, out_shape=(level, level, jax.ShapeDtypeStruct...  61.8 us

profile of v5, /device:TPU:0, one launch (start us, length us, event | category | flops | bytes accessed | tf_op | source)
XLA Modules:
  0.0 63.9 jit_solution(2745921893789440970)
XLA Ops:
  0.6 0.0 copy-start.1
  0.6 0.0 copy-start
  0.7 0.0 copy-start.4
  0.7 0.0 copy-start.5
  0.7 0.0 copy-start.6
  0.7 61.8 %plan.1 = (f32[16,128]{1,0:T(8,128)S(1)}, f32[16,128]{1,0:T(8,128)S(1)}, s32[1,1]{1,0:T(1,128)}) custom-call(s32[16,32]{1,0:T(8,128)} %support_in.1, bf16[16,64,128]{2,1,0:T(8,128)(2,1)} %source_in.1, bf16[16,64,128]{2,1,0:T(8,128)(2,1)} %target_in.1, f32[16,128]{1,0:T(8,128)} %mass_in.1, f32[16,128]{1,0:T(8,128)} %target_mass_in.1, f32[16,128]{1,0:T(8,128)} %coarse_in.1), custom_call_target="tpu_custom_call" | custom-call | tf_op jit(solution)/shard_map/plan/pallas_call | solution.py:809
  62.5 0.0 copy-start.3
  63.3 0.0 copy-done.1
  63.3 0.0 copy-done
  63.3 0.0 copy-done.4
  63.3 0.0 copy-done.5
  63.3 0.0 copy-done.6
  63.3 0.0 copy-done.3
  63.3 0.6 broadcast_multiply_fusion
  (1 shorter events, 0.0 us)
Async XLA Ops:
  0.6 62.6 %copy-start.1 = (bf16[16,64,128]{2,1,0:T(8,128)(2,1)S(1)}, bf16[16,64,128]{2,1,0:T(8,128)(2,1)}, u32[]{:S(2)}) copy-start(bf16[16,64,128]{2,1,0:T(8,128)(2,1)} %source_in.1) | copy-start | bytes 786436
  0.6 62.6 %copy-start = (bf16[16,64,128]{2,1,0:T(8,128)(2,1)S(1)}, bf16[16,64,128]{2,1,0:T(8,128)(2,1)}, u32[]{:S(2)}) copy-start(bf16[16,64,128]{2,1,0:T(8,128)(2,1)} %target_in.1) | copy-start | bytes 786436
  0.7 62.6 %copy-start.4 = (f32[16,128]{1,0:T(8,128)S(1)}, f32[16,128]{1,0:T(8,128)}, u32[]{:S(2)}) copy-start(f32[16,128]{1,0:T(8,128)} %target_mass_in.1) | copy-start | bytes 24580
  0.7 62.6 %copy-start.5 = (f32[16,128]{1,0:T(8,128)S(1)}, f32[16,128]{1,0:T(8,128)}, u32[]{:S(2)}) copy-start(f32[16,128]{1,0:T(8,128)} %coarse_in.1) | copy-start | bytes 24580
  0.7 62.6 %copy-start.6 = (f32[16,128]{1,0:T(8,128)S(1)}, f32[16,128]{1,0:T(8,128)}, u32[]{:S(2)}) copy-start(f32[16,128]{1,0:T(8,128)} %mass_in.1) | copy-start | bytes 24580
  62.5 0.8 %copy-start.3 = (s32[16,32]{1,0:T(8,128)S(1)}, s32[16,32]{1,0:T(8,128)}, u32[]{:S(2)}) copy-start(s32[16,32]{1,0:T(8,128)} %support_in.1) | copy-start | bytes 6148
